TPU v7x, 8 devices: a whole 2x2x1 slice. The times are simulated.
8 devices in a mesh: data: 1 (over z), expert: 8 (over y, x, core).
Axes of the slice: x: 2, y: 2, z: 1, core: 2. Of those that a mesh axis runs over, the one named last changes fastest.
Arguments:
- x_tokens: bfloat16 [512, 1536], P(('data', 'expert'))
- y_mid: bfloat16 [512, 1536], P(('data', 'expert'))
- dy_out: bfloat16 [512, 1536], P(('data', 'expert'))
- experts_one: int32 [512, 8], P(('data', 'expert'))
- gates_one: float32 [512, 8], P(('data', 'expert'))
- slots_one: int32 [512, 8], P(('data', 'expert'))
- experts_two: int32 [512, 8], P(('data', 'expert'))
- gates_two: float32 [512, 8], P(('data', 'expert'))
- slots_two: int32 [512, 8], P(('data', 'expert'))
- w_gate_one: bfloat16 [40, 1536, 512], P('expert')
- w_up_one: bfloat16 [40, 1536, 512], P('expert')
- w_down_one: bfloat16 [40, 512, 1536], P('expert')
- w_gate_two: bfloat16 [40, 1536, 512], P('expert')
- w_up_two: bfloat16 [40, 1536, 512], P('expert')
- w_down_two: bfloat16 [40, 512, 1536], P('expert')
Outputs:
- output 1: bfloat16 [512, 1536], P(('data', 'expert'))
- output 2: float32 [40, 1536, 512], P(('data', 'expert'))
- output 3: float32 [40, 1536, 512], P(('data', 'expert'))
- output 4: float32 [40, 512, 1536], P(('data', 'expert'))
- output 5: float32 [40, 1536, 512], P(('data', 'expert'))
- output 6: float32 [40, 1536, 512], P(('data', 'expert'))
- output 7: float32 [40, 512, 1536], P(('data', 'expert'))
All inputs are finite; a program needn't handle non-finite values.
Results may differ from a plain program's by a relative error of at most 0.0132769.
Values are sent between devices in bfloat16 or wider.
A program may use at most 1 GiB of HBM per device.

v0:
```python
import functools
import jax
import jax.numpy as jnp
from jax import lax
from jax.sharding import PartitionSpec as P


def slot_capacity(tokens_dev, top_k, n_experts):
    return 8 * ((3 * top_k * tokens_dev + 16 * n_experts - 1) // (16 * n_experts))


def route_matrix(experts, slots, gates, n_experts, capacity):
    target = jnp.where(slots >= 0, experts * capacity + slots, -1)
    slot_ids = lax.broadcasted_iota(jnp.int32, (n_experts * capacity, 1), 0)
    matches = [slot_ids == target[None, :, choice] for choice in range(experts.shape[1])]
    send_mat = functools.reduce(jnp.logical_or, matches).astype(jnp.bfloat16)
    gate_terms = [jnp.sum(jnp.where(matches[choice], gates[None, :, choice], 0.0), axis=1) for choice in range(experts.shape[1])]
    return send_mat, functools.reduce(jnp.add, gate_terms)


def expert_grads(x_rows, dz_rows, w_gate, w_up, w_down):
    gate_act = jnp.einsum("erd,edf->erf", x_rows, w_gate, preferred_element_type=jnp.float32).astype(jnp.bfloat16)
    up_act = jnp.einsum("erd,edf->erf", x_rows, w_up, preferred_element_type=jnp.float32).astype(jnp.bfloat16)
    gate_wide = gate_act.astype(jnp.float32)
    up_wide = up_act.astype(jnp.float32)
    sig_gate = jax.nn.sigmoid(gate_wide)
    silu_gate = gate_wide * sig_gate
    hidden = (silu_gate * up_wide).astype(jnp.bfloat16)
    d_hidden = jnp.einsum("erd,efd->erf", dz_rows, w_down, preferred_element_type=jnp.float32)
    dw_down = jnp.einsum("erf,erd->efd", hidden, dz_rows, preferred_element_type=jnp.float32)
    d_gate = (d_hidden * up_wide * sig_gate * (1.0 + gate_wide * (1.0 - sig_gate))).astype(jnp.bfloat16)
    d_up = (d_hidden * silu_gate).astype(jnp.bfloat16)
    dx_rows = (jnp.einsum("erf,edf->erd", d_gate, w_gate, preferred_element_type=jnp.float32) + jnp.einsum("erf,edf->erd", d_up, w_up, preferred_element_type=jnp.float32)).astype(jnp.bfloat16)
    dw_gate = jnp.einsum("erd,erf->edf", x_rows, d_gate, preferred_element_type=jnp.float32)
    dw_up = jnp.einsum("erd,erf->edf", x_rows, d_up, preferred_element_type=jnp.float32)
    return dx_rows, dw_gate, dw_up, dw_down


def layer_backward(inputs, cotangent, experts, gates, slots, w_gate, w_up, w_down, group_size):
    tokens_dev, model_dim = inputs.shape
    n_experts = w_gate.shape[0] * group_size
    capacity = slot_capacity(tokens_dev, experts.shape[1], n_experts)
    send_mat, slot_gate = route_matrix(experts, slots, gates, n_experts, capacity)
    x_send = jnp.dot(send_mat, inputs, preferred_element_type=jnp.float32).astype(jnp.bfloat16)
    dy_send = jnp.dot(send_mat, cotangent, preferred_element_type=jnp.float32)
    z_send = (slot_gate[:, None] * dy_send).astype(jnp.bfloat16)
    x_rows = lax.all_to_all(x_send.reshape(n_experts, capacity, model_dim), "expert", 0, 1, tiled=True)
    dz_rows = lax.all_to_all(z_send.reshape(n_experts, capacity, model_dim), "expert", 0, 1, tiled=True)
    dx_rows, dw_gate, dw_up, dw_down = expert_grads(x_rows, dz_rows, w_gate, w_up, w_down)
    returned = lax.all_to_all(dx_rows, "expert", 1, 0, tiled=True).reshape(n_experts * capacity, model_dim)
    summed = jnp.einsum("rt,rd->td", send_mat, returned, preferred_element_type=jnp.float32)
    return summed, dw_gate, dw_up, dw_down


def solution(mesh):
    group_size = mesh.shape["expert"]
    tok_spec = P(("data", "expert"), None)
    weight_spec = P("expert", None, None)
    grad_spec = P(("data", "expert"), None, None)

    def local_step(x_tokens, y_mid, dy_out, experts_one, gates_one, slots_one, experts_two, gates_two, slots_two, w_gate_one, w_up_one, w_down_one, w_gate_two, w_up_two, w_down_two):
        grads_two = layer_backward(y_mid, dy_out, experts_two, gates_two, slots_two, w_gate_two, w_up_two, w_down_two, group_size)
        dy_mid = (dy_out.astype(jnp.float32) + grads_two[0]).astype(jnp.bfloat16)
        grads_one = layer_backward(x_tokens, dy_mid, experts_one, gates_one, slots_one, w_gate_one, w_up_one, w_down_one, group_size)
        dx_tokens = (dy_mid.astype(jnp.float32) + grads_one[0]).astype(jnp.bfloat16)
        return (dx_tokens,) + grads_one[1:] + grads_two[1:]

    return jax.shard_map(local_step, mesh=mesh, in_specs=(tok_spec,) * 9 + (weight_spec,) * 6, out_specs=(tok_spec,) + (grad_spec,) * 6, check_vma=False)
```

profile of v0, /device:TPU:0, one launch (start us, length us, event | category | flops | bytes accessed | tf_op | source)
XLA Modules:
  0.0 322.4 jit_solution(18383720286108604713)
XLA Ops:
  0.6 0.7 add_select_fusion.1
  1.4 1.0 slice_bitcast_fusion.22
  2.5 0.1 select_reduce_fusion.10
  3.0 3.6 %multiply_convert_fusion.1 = bf16[960,1536]{1,0:T(8,128)(2,1)} fusion(bf16[64,1536]{1,0:T(8,128)(2,1)} %param.17, f32[960]{0:T(1024)S(1)} %add_add_fusion.1, s32[64]{0:T(128)S(1)} %get-tuple-element.24, s32[64]{0:T(128)S(1)} %get-tuple-element.25, s32[64]{0:T(128)S(1)} %get-tuple-element.26, s32[64]{0:T(128)S(1)} %get-tuple-element.27, ...), kind=kOutput, calls=%fused_computation.3 | convolution fusion | flops 192614400 | bytes 3151616 | tf_op jit(solution)/shard_map/dot_general | solution.py:45
  6.6 4.3 %all-to-all-start = ((bf16[40,24,1536]{2,1,0:T(8,128)(2,1)}), bf16[40,24,1536]{2,1,0:T(8,128)(2,1)S(1)}, u32[]{:S(2)}, u32[]{:S(2)}) async-start(bf16[40,24,1536]{2,1,0:T(8,128)(2,1)} %bitcast.147), calls=%async_computation | async-start | bytes 5898240 | tf_op jit(solution)/shard_map/all_to_all | solution.py:48
  10.9 2.7 convolution_convert_fusion.1
  13.7 33.0 %all-to-all-done = bf16[40,24,1536]{2,1,0:T(8,128)(2,1)S(1)} async-done(((bf16[40,24,1536]{2,1,0:T(8,128)(2,1)}), bf16[40,24,1536]{2,1,0:T(8,128)(2,1)S(1)}, u32[]{:S(2)}, u32[]{:S(2)}) %all-to-all-start) | async-done | bytes 2949152 | tf_op jit(solution)/shard_map/all_to_all | solution.py:48
  46.7 1.6 copy-done.9
  48.3 2.4 all-to-all-start.1
  50.7 2.7 convolution_convert_fusion
  53.4 1.9 copy.48
  55.3 31.0 %all-to-all-done.1 = bf16[40,24,1536]{2,1,0:T(8,128)(2,1)S(1)} async-done(((bf16[40,24,1536]{2,1,0:T(8,128)(2,1)}), bf16[40,24,1536]{2,1,0:T(8,128)(2,1)S(1)}, u32[]{:S(2)}, u32[]{:S(2)}) %all-to-all-start.1) | async-done | bytes 2949152 | tf_op jit(solution)/shard_map/all_to_all | solution.py:47
  86.3 1.6 copy-done.8
  87.9 3.6 %all-to-all-start.4 = ((bf16[40,24,1536]{2,1,0:T(8,128)(2,1)}), bf16[40,24,1536]{2,1,0:T(8,128)(2,1)}, u32[]{:S(2)}, u32[]{:S(2)}) async-start(bf16[40,24,1536]{2,1,0:T(8,128)(2,1)} %bitcast.143), calls=%async_computation.4 | async-start | bytes 5898240 | tf_op jit(solution)/shard_map/all_to_all | solution.py:47
  91.6 2.3 copy.49
  93.9 5.1 %convolution_convert_fusion.4 = bf16[5,192,512]{2,1,0:T(8,128)(2,1)S(1)} fusion(bf16[5,192,1536]{2,1,0:T(8,128)(2,1)S(1)} %bitcast.124, bf16[5,1536,512]{2,1,0:T(8,128)(2,1)} %param.27), kind=kOutput, calls=%fused_computation.40 | convolution fusion | flops 1510440960 | bytes 11796480 | tf_op jit(solution)/shard_map/erd,edf->erf/dot_general | solution.py:22
  99.0 1.7 convolution_convert_fusion.5
  100.7 0.4 copy-done.4
  101.2 7.9 %fusion.4 = (bf16[5,192,512]{2,1,0:T(8,128)(2,1)S(1)}, f32[5,192,512]{2,1,0:T(8,128)}) fusion(bf16[5,192,512]{2,1,0:T(8,128)(2,1)S(1)} %convolution_convert_fusion.5, bf16[5,192,512]{2,1,0:T(8,128)(2,1)S(1)} %convolution_convert_fusion.4, bf16[5,192,1536]{2,1,0:T(8,128)(2,1)S(1)} %bitcast.136, bf16[5,512,1536]{2,1,0:T(8,128)(2,1)} %param.29), kind=kOutput, calls=%fused_computation.22 | convolution fusion | flops 1515847680 | bytes 15728640 | tf_op jit(solution)/shard_map/erd,efd->erf/dot_general | solution.py:29
  109.1 2.7 fusion.46
  111.8 8.3 %add_convert_fusion.1 = bf16[5,192,1536]{2,1,0:T(8,128)(2,1)} fusion(f32[5,192,1536]{2,1,0:T(8,128)S(1)} %fusion.46, bf16[5,1536,512]{2,1,0:T(8,128)(2,1)} %param.28, f32[5,192,512]{2,1,0:T(8,128)} %get-tuple-element.40, bf16[5,192,512]{2,1,0:T(8,128)(2,1)S(1)} %convolution_convert_fusion.4), kind=kOutput, calls=%fused_computation.2 | convolution fusion | flops 1516339200 | bytes 19660800 | tf_op jit(solution)/shard_map/erf,edf->erd/dot_general | solution.py:33
  120.1 5.8 %copy.50 = bf16[5,192,1536]{2,0,1:T(8,128)(2,1)} copy(bf16[5,192,1536]{2,1,0:T(8,128)(2,1)} %add_convert_fusion.1) | data formatting | bytes 5898240 | tf_op jit(solution)/shard_map/convert_element_type | solution.py:33
  125.9 1.3 all-to-all-done.4
  127.2 3.5 %all-to-all-start.2 = ((bf16[5,192,1536]{2,0,1:T(8,128)(2,1)}), bf16[5,192,1536]{2,0,1:T(8,128)(2,1)}, u32[]{:S(2)}, u32[]{:S(2)}) async-start(bf16[5,192,1536]{2,0,1:T(8,128)(2,1)} %copy.50), calls=%async_computation.2 | async-start | bytes 9437184 | tf_op jit(solution)/shard_map/all_to_all | solution.py:50
  131.4 3.7 %copy.54 = bf16[8,5,24,1536]{3,2,0,1:T(8,128)(2,1)} copy(bf16[8,5,24,1536]{3,2,1,0:T(8,128)(2,1)} %bitcast.50) | data formatting | bytes 5898240 | tf_op jit(solution)/shard_map/all_to_all | solution.py:47
  135.1 50.3 %all-to-all-done.2 = bf16[5,192,1536]{2,0,1:T(8,128)(2,1)} async-done(((bf16[5,192,1536]{2,0,1:T(8,128)(2,1)}), bf16[5,192,1536]{2,0,1:T(8,128)(2,1)}, u32[]{:S(2)}, u32[]{:S(2)}) %all-to-all-start.2) | async-done | bytes 2949152 | tf_op jit(solution)/shard_map/all_to_all | solution.py:50
  185.4 3.5 %copy.52 = bf16[8,5,24,1536]{3,2,1,0:T(8,128)(2,1)S(1)} copy(bf16[8,5,24,1536]{3,1,2,0:T(8,128)(2,1)} %bitcast.27) | data formatting | bytes 5898240 | tf_op jit(solution)/shard_map/all_to_all | solution.py:50
  188.9 0.8 fusion
  189.7 2.7 multiply_convert_fusion
  192.4 3.2 all-to-all-start.3
  195.6 6.9 %convolution_convert_fusion.2 = bf16[5,192,512]{2,1,0:T(8,128)(2,1)} fusion(bf16[5,192,1536]{2,1,0:T(8,128)(2,1)} %bitcast.128, bf16[5,1536,512]{2,1,0:T(8,128)(2,1)} %param.24), kind=kOutput, calls=%fused_computation.38 | convolution fusion | flops 1510440960 | bytes 11796480 | tf_op jit(solution)/shard_map/erd,edf->erf/dot_general | solution.py:22
  202.6 6.1 %convolution_convert_fusion.3 = bf16[5,192,512]{2,1,0:T(8,128)(2,1)} fusion(bf16[5,192,1536]{2,1,0:T(8,128)(2,1)S(1)} %bitcast.129, bf16[5,1536,512]{2,1,0:T(8,128)(2,1)} %param.25), kind=kOutput, calls=%fused_computation.39 | convolution fusion | flops 1510440960 | bytes 11796480 | tf_op jit(solution)/shard_map/erd,edf->erf/dot_general | solution.py:23
  208.7 8.1 %fusion.20 = f32[5,512,1536]{2,1,0:T(8,128)} fusion(bf16[5,192,1536]{2,1,0:T(8,128)(2,1)S(1)} %bitcast.137, bf16[5,192,512]{2,1,0:T(8,128)(2,1)S(1)} %copy-done.21, bf16[5,192,512]{2,1,0:T(8,128)(2,1)S(1)} %copy-done.15), kind=kOutput, calls=%fused_computation.43 | convolution fusion | flops 1513881600 | bytes 20643840 | tf_op jit(solution)/shard_map/erf,erd->efd/dot_general | solution.py:30
  216.8 8.1 %fusion.44 = f32[5,1536,512]{2,1,0:T(8,128)} fusion(bf16[5,192,1536]{2,1,0:T(8,128)(2,1)S(1)} %bitcast.126, f32[5,192,512]{2,1,0:T(8,128)S(1)} %copy-done.18, bf16[5,192,512]{2,1,0:T(8,128)(2,1)S(1)} %copy-done.15), kind=kOutput, calls=%fused_computation.128 | convolution fusion | flops 1513390080 | bytes 21626880 | tf_op jit(solution)/shard_map/erd,erf->edf/dot_general | solution.py:35
  224.9 6.3 %all-to-all-done.3 = bf16[40,24,1536]{2,1,0:T(8,128)(2,1)} async-done(((bf16[40,24,1536]{2,1,0:T(8,128)(2,1)}), bf16[40,24,1536]{2,1,0:T(8,128)(2,1)}, u32[]{:S(2)}, u32[]{:S(2)}) %all-to-all-start.3) | async-done | bytes 2949152 | tf_op jit(solution)/shard_map/all_to_all | solution.py:48
  231.3 2.3 copy.53
  233.6 8.7 %fusion.8 = (bf16[5,192,512]{2,1,0:T(8,128)(2,1)S(1)}, f32[5,192,512]{2,1,0:T(8,128)}) fusion(bf16[5,192,512]{2,1,0:T(8,128)(2,1)} %convolution_convert_fusion.3, bf16[5,192,512]{2,1,0:T(8,128)(2,1)S(1)} %copy-done.16, bf16[5,192,1536]{2,1,0:T(8,128)(2,1)S(1)} %bitcast.138, bf16[5,512,1536]{2,1,0:T(8,128)(2,1)} %param.26), kind=kOutput, calls=%fused_computation.26 | convolution fusion | flops 1515847680 | bytes 15728640 | tf_op jit(solution)/shard_map/erd,efd->erf/dot_general | solution.py:29
  242.3 2.7 fusion.47
  245.0 8.5 %add_convert_fusion = bf16[5,192,1536]{2,1,0:T(8,128)(2,1)} fusion(f32[5,192,1536]{2,1,0:T(8,128)S(1)} %fusion.47, bf16[5,1536,512]{2,1,0:T(8,128)(2,1)} %param.25, f32[5,192,512]{2,1,0:T(8,128)} %get-tuple-element.42, bf16[5,192,512]{2,1,0:T(8,128)(2,1)S(1)} %copy-done.16), kind=kOutput, calls=%fused_computation | convolution fusion | flops 1516339200 | bytes 19660800 | tf_op jit(solution)/shard_map/erf,edf->erd/dot_general | solution.py:33
  253.5 5.7 %copy.55 = bf16[5,192,1536]{2,0,1:T(8,128)(2,1)} copy(bf16[5,192,1536]{2,1,0:T(8,128)(2,1)} %add_convert_fusion) | data formatting | bytes 5898240 | tf_op jit(solution)/shard_map/convert_element_type | solution.py:33
  259.2 3.3 %all-to-all-start.5 = ((bf16[5,192,1536]{2,0,1:T(8,128)(2,1)}), bf16[5,192,1536]{2,0,1:T(8,128)(2,1)}, u32[]{:S(2)}, u32[]{:S(2)}) async-start(bf16[5,192,1536]{2,0,1:T(8,128)(2,1)} %copy.55), calls=%async_computation.5 | async-start | bytes 9437184 | tf_op jit(solution)/shard_map/all_to_all | solution.py:50
  262.6 9.5 %fusion.49 = f32[5,1536,512]{2,1,0:T(8,128)} fusion(bf16[5,192,1536]{2,1,0:T(8,128)(2,1)S(1)} %bitcast.127, bf16[5,192,512]{2,1,0:T(8,128)(2,1)} %copy-done.11), kind=kOutput, calls=%fused_computation.133 | convolution fusion | flops 1509949440 | bytes 19660800 | tf_op jit(solution)/shard_map/erd,erf->edf/dot_general | solution.py:34
  272.1 8.1 %fusion.48 = f32[5,1536,512]{2,1,0:T(8,128)} fusion(bf16[5,192,1536]{2,1,0:T(8,128)(2,1)S(1)} %bitcast.130, bf16[5,192,512]{2,1,0:T(8,128)(2,1)S(1)} %copy-done.13), kind=kOutput, calls=%fused_computation.132 | convolution fusion | flops 1509949440 | bytes 19660800 | tf_op jit(solution)/shard_map/erd,erf->edf/dot_general | solution.py:34
  280.3 8.1 %fusion.18 = f32[5,512,1536]{2,1,0:T(8,128)} fusion(bf16[5,192,1536]{2,1,0:T(8,128)(2,1)S(1)} %bitcast.139, bf16[5,192,512]{2,1,0:T(8,128)(2,1)S(1)} %copy-done.22, bf16[5,192,512]{2,1,0:T(8,128)(2,1)S(1)} %copy-done.17), kind=kOutput, calls=%fused_computation.42 | convolution fusion | flops 1513881600 | bytes 20643840 | tf_op jit(solution)/shard_map/erf,erd->efd/dot_general | solution.py:30
  288.4 8.1 %fusion.45 = f32[5,1536,512]{2,1,0:T(8,128)} fusion(bf16[5,192,1536]{2,1,0:T(8,128)(2,1)S(1)} %bitcast.131, f32[5,192,512]{2,1,0:T(8,128)S(1)} %copy-done.19, bf16[5,192,512]{2,1,0:T(8,128)(2,1)S(1)} %copy-done.17), kind=kOutput, calls=%fused_computation.129 | convolution fusion | flops 1513390080 | bytes 21626880 | tf_op jit(solution)/shard_map/erd,erf->edf/dot_general | solution.py:35
  296.5 20.7 %all-to-all-done.5 = bf16[5,192,1536]{2,0,1:T(8,128)(2,1)} async-done(((bf16[5,192,1536]{2,0,1:T(8,128)(2,1)}), bf16[5,192,1536]{2,0,1:T(8,128)(2,1)}, u32[]{:S(2)}, u32[]{:S(2)}) %all-to-all-start.5) | async-done | bytes 2949152 | tf_op jit(solution)/shard_map/all_to_all | solution.py:50
  317.2 3.5 %copy.57 = bf16[8,5,24,1536]{3,2,1,0:T(8,128)(2,1)S(1)} copy(bf16[8,5,24,1536]{3,1,2,0:T(8,128)(2,1)} %bitcast.56) | data formatting | bytes 5898240 | tf_op jit(solution)/shard_map/all_to_all | solution.py:50
  320.7 1.5 fusion.1
  (81 shorter events, 1.2 us)
Async XLA Ops:
  0.6 10.3 %copy-start = (bf16[64,1536]{1,0:T(8,128)(2,1)S(1)}, bf16[64,1536]{1,0:T(8,128)(2,1)}, u32[]{:S(2)}) copy-start(bf16[64,1536]{1,0:T(8,128)(2,1)} %param.16) | copy-start | bytes 589828
  6.6 40.0 %all-to-all-start = ((bf16[40,24,1536]{2,1,0:T(8,128)(2,1)}), bf16[40,24,1536]{2,1,0:T(8,128)(2,1)S(1)}, u32[]{:S(2)}, u32[]{:S(2)}) async-start(bf16[40,24,1536]{2,1,0:T(8,128)(2,1)} %bitcast.147), calls=%async_computation | async-start | bytes 5898240 | tf_op jit(solution)/shard_map/all_to_all | solution.py:48
  46.7 1.6 copy-start.9
  46.7 4.0 %copy-start.25 = (s32[64,8]{0,1:T(8,128)S(1)}, s32[64,8]{0,1:T(8,128)}, u32[]{:S(2)}) copy-start(s32[64,8]{0,1:T(8,128)} %param.20) | copy-start | bytes 6148
  46.7 4.0 %copy-start.26 = (s32[64,8]{0,1:T(8,128)S(1)}, s32[64,8]{0,1:T(8,128)}, u32[]{:S(2)}) copy-start(s32[64,8]{0,1:T(8,128)} %param.18) | copy-start | bytes 6148
  46.7 4.0 %copy-start.23 = (bf16[64,1536]{1,0:T(8,128)(2,1)S(1)}, bf16[64,1536]{1,0:T(8,128)(2,1)}, u32[]{:S(2)}) copy-start(bf16[64,1536]{1,0:T(8,128)(2,1)} %param.15) | copy-start | bytes 589828
  48.3 38.1 %all-to-all-start.1 = ((bf16[40,24,1536]{2,1,0:T(8,128)(2,1)}), bf16[40,24,1536]{2,1,0:T(8,128)(2,1)S(1)}, u32[]{:S(2)}, u32[]{:S(2)}) async-start(bf16[40,24,1536]{2,1,0:T(8,128)(2,1)} %bitcast.142), calls=%async_computation.1 | async-start | bytes 5898240 | tf_op jit(solution)/shard_map/all_to_all | solution.py:47
  50.7 2.8 copy-start.10
  86.3 1.6 copy-start.8
  87.9 39.3 %all-to-all-start.4 = ((bf16[40,24,1536]{2,1,0:T(8,128)(2,1)}), bf16[40,24,1536]{2,1,0:T(8,128)(2,1)}, u32[]{:S(2)}, u32[]{:S(2)}) async-start(bf16[40,24,1536]{2,1,0:T(8,128)(2,1)} %bitcast.143), calls=%async_computation.4 | async-start | bytes 5898240 | tf_op jit(solution)/shard_map/all_to_all | solution.py:47
  91.6 7.4 %slice-start.4 = ((s8[7864320]{0:T(1024)(128)(4,1)}), s8[4194304]{0:T(1024)(128)(4,1)S(1)}, s32[]{:S(2)}) async-start(s8[7864320]{0:T(1024)(128)(4,1)} %bitcast.148), calls=%async_computation.10 | async-start | bytes 8388608
  93.8 5.1 %slice-start.5 = ((s8[7864320]{0:T(1024)(128)(4,1)}), s8[3670016]{0:T(1024)(128)(4,1)S(1)}, s32[]{:S(2)}) async-start(s8[7864320]{0:T(1024)(128)(4,1)} %bitcast.148), calls=%async_computation.11 | async-start | bytes 7340032
  99.0 12.9 %copy-start.14 = (bf16[5,192,512]{2,1,0:T(8,128)(2,1)}, bf16[5,192,512]{2,1,0:T(8,128)(2,1)S(1)}, u32[]{:S(2)}) copy-start(bf16[5,192,512]{2,1,0:T(8,128)(2,1)S(1)} %convolution_convert_fusion.4) | copy-start | bytes 2949124
  99.0 2.2 copy-start.4
  99.0 10.1 %slice-start = ((s8[7864320]{0:T(1024)(128)(4,1)}), s8[4194304]{0:T(1024)(128)(4,1)S(1)}, s32[]{:S(2)}) async-start(s8[7864320]{0:T(1024)(128)(4,1)} %bitcast.132), calls=%async_computation.6 | async-start | bytes 8388608
  100.7 8.4 %copy-start.20 = (bf16[5,192,512]{2,1,0:T(8,128)(2,1)}, bf16[5,192,512]{2,1,0:T(8,128)(2,1)S(1)}, u32[]{:S(2)}) copy-start(bf16[5,192,512]{2,1,0:T(8,128)(2,1)S(1)} %convolution_convert_fusion.5) | copy-start | bytes 2949124
  101.2 7.9 %slice-start.1 = ((s8[7864320]{0:T(1024)(128)(4,1)}), s8[3670016]{0:T(1024)(128)(4,1)S(1)}, s32[]{:S(2)}) async-start(s8[7864320]{0:T(1024)(128)(4,1)} %bitcast.132), calls=%async_computation.7 | async-start | bytes 7340032
  109.1 2.8 copy-start.11
  125.9 4.9 %copy-start.27 = (f32[64,8]{0,1:T(8,128)S(1)}, f32[64,8]{0,1:T(8,128)}, u32[]{:S(2)}) copy-start(f32[64,8]{0,1:T(8,128)} %param.19) | copy-start | bytes 6148
  127.2 58.2 %all-to-all-start.2 = ((bf16[5,192,1536]{2,0,1:T(8,128)(2,1)}), bf16[5,192,1536]{2,0,1:T(8,128)(2,1)}, u32[]{:S(2)}, u32[]{:S(2)}) async-start(bf16[5,192,1536]{2,0,1:T(8,128)(2,1)} %copy.50), calls=%async_computation.2 | async-start | bytes 9437184 | tf_op jit(solution)/shard_map/all_to_all | solution.py:50
  185.4 3.5 %copy-start.24 = (bf16[64,1536]{1,0:T(8,128)(2,1)S(1)}, bf16[64,1536]{1,0:T(8,128)(2,1)}, u32[]{:S(2)}) copy-start(bf16[64,1536]{1,0:T(8,128)(2,1)} %param.17) | copy-start | bytes 589828
  192.4 38.8 %all-to-all-start.3 = ((bf16[40,24,1536]{2,1,0:T(8,128)(2,1)}), bf16[40,24,1536]{2,1,0:T(8,128)(2,1)}, u32[]{:S(2)}, u32[]{:S(2)}) async-start(bf16[40,24,1536]{2,1,0:T(8,128)(2,1)} %bitcast.146), calls=%async_computation.3 | async-start | bytes 5898240 | tf_op jit(solution)/shard_map/all_to_all | solution.py:48
  195.6 6.9 %copy-start.2 = (bf16[8,5,24,1536]{3,2,0,1:T(8,128)(2,1)S(1)}, bf16[8,5,24,1536]{3,2,0,1:T(8,128)(2,1)}, u32[]{:S(2)}) copy-start(bf16[8,5,24,1536]{3,2,0,1:T(8,128)(2,1)} %copy.54) | copy-start | bytes 8847364
  202.5 6.1 %copy-start.5 = (bf16[8,5,24,1536]{3,2,0,1:T(8,128)(2,1)S(1)}, bf16[8,5,24,1536]{3,2,0,1:T(8,128)(2,1)}, u32[]{:S(2)}) copy-start(bf16[8,5,24,1536]{3,2,0,1:T(8,128)(2,1)} %copy.48) | copy-start | bytes 8847364
  202.6 6.1 %copy-start.15 = (bf16[5,192,512]{2,1,0:T(8,128)(2,1)S(1)}, bf16[5,192,512]{2,1,0:T(8,128)(2,1)}, u32[]{:S(2)}) copy-start(bf16[5,192,512]{2,1,0:T(8,128)(2,1)} %copy-done.14) | copy-start | bytes 2949124
  202.6 6.1 %copy-start.21 = (bf16[5,192,512]{2,1,0:T(8,128)(2,1)S(1)}, bf16[5,192,512]{2,1,0:T(8,128)(2,1)}, u32[]{:S(2)}) copy-start(bf16[5,192,512]{2,1,0:T(8,128)(2,1)} %copy-done.20) | copy-start | bytes 2949124
  208.7 8.1 %copy-start.18 = (f32[5,192,512]{2,1,0:T(8,128)S(1)}, f32[5,192,512]{2,1,0:T(8,128)}, u32[]{:S(2)}) copy-start(f32[5,192,512]{2,1,0:T(8,128)} %get-tuple-element.40) | copy-start | bytes 5898244
  231.3 2.3 copy-start.16
  231.3 11.0 %slice-start.2 = ((s8[7864320]{0:T(1024)(128)(4,1)}), s8[4194304]{0:T(1024)(128)(4,1)S(1)}, s32[]{:S(2)}) async-start(s8[7864320]{0:T(1024)(128)(4,1)} %bitcast.134), calls=%async_computation.8 | async-start | bytes 8388608
  233.5 8.7 %copy-start.6 = (bf16[8,5,24,1536]{3,2,0,1:T(8,128)(2,1)}, bf16[8,5,24,1536]{3,2,0,1:T(8,128)(2,1)S(1)}, u32[]{:S(2)}) copy-start(bf16[8,5,24,1536]{3,2,0,1:T(8,128)(2,1)S(1)} %copy.53) | copy-start | bytes 8847364
  233.6 8.7 %slice-start.3 = ((s8[7864320]{0:T(1024)(128)(4,1)}), s8[3670016]{0:T(1024)(128)(4,1)S(1)}, s32[]{:S(2)}) async-start(s8[7864320]{0:T(1024)(128)(4,1)} %bitcast.134), calls=%async_computation.9 | async-start | bytes 7340032
  242.3 2.8 copy-start.12
  259.2 58.0 %all-to-all-start.5 = ((bf16[5,192,1536]{2,0,1:T(8,128)(2,1)}), bf16[5,192,1536]{2,0,1:T(8,128)(2,1)}, u32[]{:S(2)}, u32[]{:S(2)}) async-start(bf16[5,192,1536]{2,0,1:T(8,128)(2,1)} %copy.55), calls=%async_computation.5 | async-start | bytes 9437184 | tf_op jit(solution)/shard_map/all_to_all | solution.py:50
  262.6 9.5 %copy-start.3 = (bf16[8,5,24,1536]{3,2,0,1:T(8,128)(2,1)S(1)}, bf16[8,5,24,1536]{3,2,0,1:T(8,128)(2,1)}, u32[]{:S(2)}) copy-start(bf16[8,5,24,1536]{3,2,0,1:T(8,128)(2,1)} %copy.54) | copy-start | bytes 8847364
  262.6 9.5 %copy-start.13 = (bf16[5,192,512]{2,1,0:T(8,128)(2,1)S(1)}, bf16[5,192,512]{2,1,0:T(8,128)(2,1)}, u32[]{:S(2)}) copy-start(bf16[5,192,512]{2,1,0:T(8,128)(2,1)} %copy-done.12) | copy-start | bytes 2949124
  272.1 8.2 %copy-start.7 = (bf16[8,5,24,1536]{3,2,0,1:T(8,128)(2,1)S(1)}, bf16[8,5,24,1536]{3,2,0,1:T(8,128)(2,1)}, u32[]{:S(2)}) copy-start(bf16[8,5,24,1536]{3,2,0,1:T(8,128)(2,1)} %copy-done.6) | copy-start | bytes 8847364
  272.1 8.2 %copy-start.17 = (bf16[5,192,512]{2,1,0:T(8,128)(2,1)S(1)}, bf16[5,192,512]{2,1,0:T(8,128)(2,1)}, u32[]{:S(2)}) copy-start(bf16[5,192,512]{2,1,0:T(8,128)(2,1)} %convolution_convert_fusion.2) | copy-start | bytes 2949124
  272.1 8.2 %copy-start.22 = (bf16[5,192,512]{2,1,0:T(8,128)(2,1)S(1)}, bf16[5,192,512]{2,1,0:T(8,128)(2,1)}, u32[]{:S(2)}) copy-start(bf16[5,192,512]{2,1,0:T(8,128)(2,1)} %convolution_convert_fusion.3) | copy-start | bytes 2949124
  280.3 8.1 %copy-start.19 = (f32[5,192,512]{2,1,0:T(8,128)S(1)}, f32[5,192,512]{2,1,0:T(8,128)}, u32[]{:S(2)}) copy-start(f32[5,192,512]{2,1,0:T(8,128)} %get-tuple-element.42) | copy-start | bytes 5898244
  317.2 5.0 %copy-start.1 = (bf16[64,1536]{1,0:T(8,128)(2,1)S(1)}, bf16[64,1536]{1,0:T(8,128)(2,1)}, u32[]{:S(2)}) copy-start(bf16[64,1536]{1,0:T(8,128)(2,1)} %param.16) | copy-start | bytes 589828
where the time goes:
time: 327 us; the launch traced here: 322 us
  waiting for transfers between devices  143 us (44%)
  matrix products  123 us (38%)
  local copies, waits for them, and re-layouts  33.4 us (10%)
  starting transfers between devices  20.3 us (6%)
    all_to_all x2, waiting for transfers between devices, layer_backward(): lax.all_to_all(dx_rows, 'expert', 1, 0, tiled=True)  70.9 us
    all_to_all x2, waiting for transfers between devices, layer_backward(): lax.all_to_all(z_send.reshape(n_experts, capacity, model_dim), 'expert',...  39.3 us
    all_to_all x2, waiting for transfers between devices, layer_backward(): lax.all_to_all(x_send.reshape(n_experts, capacity, model_dim), 'expert',...  32.3 us
    dot_general x2, matrix products, expert_grads(): jnp.einsum('erd,erf->edf', x_rows, d_gate, preferred_element_type=jnp.flo...  17.6 us
    dot_general x2, matrix products, expert_grads(): jnp.einsum('erf,edf->erd', d_up, w_up, preferred_element_type=jnp.float32)  16.7 us
    dot_general x2, matrix products, expert_grads(): jnp.einsum('erd,efd->erf', dz_rows, w_down, preferred_element_type=jnp.fl...  16.6 us
    dot_general x2, matrix products, expert_grads(): jnp.einsum('erd,erf->edf', x_rows, d_up, preferred_element_type=jnp.float32)  16.3 us
    dot_general x2, matrix products, expert_grads(): jnp.einsum('erf,erd->efd', hidden, dz_rows, preferred_element_type=jnp.fl...  16.2 us
  transfers between devices with their start and end apart: 6, of which 6 were waited for; matrix products, arithmetic and copies ran while one was open for 34% of the time, Pallas kernels for 0%

commit v1 on v0

v1 whole, which is shorter than its diff:
```python
import functools
import jax
import jax.numpy as jnp
from jax import lax
from jax.experimental import pallas as pl
from jax.experimental.pallas import tpu as pltpu
from jax.sharding import PartitionSpec as P

MESH = pl.DeviceIdType.MESH
F32 = jnp.float32
BF16 = jnp.bfloat16
CAP = 24
LOCAL = 5
D = 1536
F = 512
TOK = 64
HALF_ROWS = 4 * CAP
ROWS = 8 * CAP
STEP = 512


def place():
    me = lax.axis_index("expert")
    core, x, y = me % 2, (me // 2) % 2, me // 4
    ident = lambda xx, yy, cc: 4 * yy + 2 * xx + cc
    ids = {
        "me": me,
        "partner": ident(x, y, 1 - core),
        "x": ident(1 - x, y, core),
        "y": ident(x, 1 - y, core),
        "diag": ident(1 - x, 1 - y, core),
        "prim": ident(x + (1 - core) * (1 - 2 * x), y + core * (1 - 2 * y), core),
        "sec": ident(x + core * (1 - 2 * x), y + (1 - core) * (1 - 2 * y), core),
        "p_prim": ident(x + core * (1 - 2 * x), y + (1 - core) * (1 - 2 * y), 1 - core),
        "p_sec": ident(x + (1 - core) * (1 - 2 * x), y + core * (1 - 2 * y), 1 - core),
        "p_diag": ident(1 - x, 1 - y, 1 - core),
    }
    return ids, core, x, y


def barrier(ids):
    sem = pltpu.get_barrier_semaphore()
    for peer in ("partner", "x", "y"):
        pl.semaphore_signal(sem, inc=1, device_id={"expert": ids[peer]}, device_id_type=MESH)
    pl.semaphore_wait(sem, 3)


def block(ref, ident):
    return ref.at[pl.ds(pl.multiple_of(ident * TOK, TOK), TOK)]


class Gather:
    ROUTES = (("me", "partner"), ("me", "prim"), ("me", "sec"), ("prim", "sec"), ("prim", "partner"), ("sec", "partner"), ("diag", "partner"))
    ARRIVE = ("partner", "prim", "sec", "diag", "p_prim", "p_sec", "p_diag")

    def __init__(self, ids, ref, send, recv):
        self.ids, self.ref, self.send, self.recv = ids, ref, send, recv

    def copy(self, k):
        what, where = self.ROUTES[k]
        part = block(self.ref, self.ids[what])
        return pltpu.make_async_remote_copy(src_ref=part, dst_ref=part, send_sem=self.send.at[k], recv_sem=self.recv.at[k], device_id={"expert": self.ids[where]}, device_id_type=MESH)

    def arrived(self, k):
        part = block(self.ref, self.ids[self.ARRIVE[k]])
        pltpu.make_async_remote_copy(src_ref=part, dst_ref=part, send_sem=self.send.at[k], recv_sem=self.recv.at[k], device_id={"expert": self.ids["partner"]}, device_id_type=MESH).wait_recv()

    def start(self):
        for k in (1, 2, 0):
            self.copy(k).start()

    def relay_prim(self):
        self.arrived(1)
        self.copy(3).start()
        self.copy(4).start()

    def relay_rest(self):
        self.arrived(2)
        self.copy(5).start()
        self.arrived(3)
        self.copy(6).start()

    def finish(self):
        for k in (0, 4, 5, 6):
            self.arrived(k)

    def drain(self):
        for k in range(7):
            self.copy(k).wait_send()


def build_onehot(table, base, me, onehot, gate_col):
    for h in range(2):
        cols = slice(h * 256, (h + 1) * 256)
        keys = [table[base + j : base + j + 1, cols] for j in range(8)]
        gates = [table[base + 8 + j : base + 9 + j, cols] for j in range(8)]
        for e in range(LOCAL):
            row = (lax.broadcasted_iota(jnp.int32, (HALF_ROWS, 256), 0) + (e + me * LOCAL) * HALF_ROWS).astype(F32)
            gate = jnp.zeros((HALF_ROWS, 256), F32)
            hit = jnp.zeros((HALF_ROWS, 256), F32)
            for j in range(8):
                match = row == keys[j]
                gate = jnp.where(match, gates[j], gate)
                hit = jnp.where(match, 1.0, hit)
            onehot[h, e * HALF_ROWS : (e + 1) * HALF_ROWS, :] = hit.astype(BF16)
            gate_col[h, e * HALF_ROWS : (e + 1) * HALF_ROWS, :] = jnp.broadcast_to(jnp.sum(gate, axis=1, keepdims=True), (HALF_ROWS, 128))


def take_rows(onehot, tokens, rows, gate_col=None):
    for h in range(2):
        for n in range(D // STEP):
            cols = slice(n * STEP, (n + 1) * STEP)
            out = jnp.dot(onehot[h], tokens[h * 256 : (h + 1) * 256, cols], preferred_element_type=F32)
            if gate_col is not None:
                out = out * gate_col[h, :, 0:1]
            out = out.astype(BF16)
            for e in range(LOCAL):
                rows[e, h * HALF_ROWS : (h + 1) * HALF_ROWS, cols] = out[e * HALF_ROWS : (e + 1) * HALF_ROWS]


def forward_expert(e, u, w1, w3, a, b, hid):
    act = jnp.dot(u[e], w1[e], preferred_element_type=F32).astype(BF16)
    up = jnp.dot(u[e], w3[e], preferred_element_type=F32).astype(BF16)
    a[e] = act
    b[e] = up
    wide = act.astype(F32)
    hid[e] = (wide * jax.nn.sigmoid(wide) * up.astype(F32)).astype(BF16)


TRANS_B = (((1,), (1,)), ((), ()))
TRANS_A = (((0,), (0,)), ((), ()))


def backward_expert(e, z, w1, w3, w2, a, b, dxr):
    dh = lax.dot_general(z[e], w2[e], TRANS_B, preferred_element_type=F32)
    act = a[e].astype(F32)
    up = b[e].astype(F32)
    sig = jax.nn.sigmoid(act)
    da = (dh * up * sig * (1.0 + act * (1.0 - sig))).astype(BF16)
    db = (dh * (act * sig)).astype(BF16)
    a[e] = da
    b[e] = db
    for n in range(D // STEP):
        cols = slice(n * STEP, (n + 1) * STEP)
        dx = lax.dot_general(da, w1[e, cols, :], TRANS_B, preferred_element_type=F32) + lax.dot_general(db, w3[e, cols, :], TRANS_B, preferred_element_type=F32)
        dx = dx.astype(BF16)
        for h in range(2):
            dxr[h, pl.ds(pl.multiple_of(e * HALF_ROWS, HALF_ROWS), HALF_ROWS), cols] = dx[h * HALF_ROWS : (h + 1) * HALF_ROWS]


def return_sums(ids, core, x, y, onehot, dxr, sums, inbox, send, recv, outs):
    def exchange(yy, xx):
        theirs = 4 * yy + 2 * xx + (1 - core)
        return pltpu.make_async_remote_copy(src_ref=block(sums, theirs), dst_ref=inbox.at[2 * yy + xx], send_sem=send.at[2 * yy + xx], recv_sem=recv.at[2 * yy + xx], device_id={"expert": ids["partner"]}, device_id_type=MESH)

    for h in range(2):
        for n in range(D // STEP):
            cols = slice(n * STEP, (n + 1) * STEP)
            sums[h * 256 : (h + 1) * 256, cols] = lax.dot_general(onehot[h], dxr[h, :, cols], TRANS_A, preferred_element_type=F32)
        for xx in range(2):
            exchange(h, xx).start()
    for h in range(2):
        for xx in range(2):
            exchange(h, xx).wait_recv()
    for name, xx, yy, out in (("me", x, y, outs[0]), ("x", 1 - x, y, outs[1]), ("y", x, 1 - y, outs[2]), ("diag", 1 - x, 1 - y, outs[3])):
        out[...] = block(sums, ids[name])[...] + inbox[2 * yy + xx]
    for h in range(2):
        for xx in range(2):
            exchange(h, xx).wait_send()


def fetch_weights(hbm, vmem, sems):
    copies = []
    for e in range(LOCAL):
        for k in range(3):
            copies.append(pltpu.make_async_copy(hbm[k].at[e], vmem[k].at[e], sems.at[k, e]))
    return copies


def layer_two_kernel(tab_h, y_h, dy_h, x_h, w1_h, w3_h, w2_h,
                     u_o, z_o, hid_o, da_o, db_o, xall_o, table_o, s_me, s_x, s_y, s_d,
                     tab, yall, dall, xall, w1, w3, w2, onehot, gate_col, u, z, a, b, hid, dxr, sums, inbox,
                     lsem, wsem, osem, gsend, grecv, xsend, xrecv):
    ids, core, x, y = place()
    local = [pltpu.make_async_copy(src, block(dst, ids["me"]), lsem.at[i]) for i, (src, dst) in enumerate(((tab_h, tab), (y_h, yall), (dy_h, dall), (x_h, xall)))]
    for c in local:
        c.start()
    weights = fetch_weights((w1_h, w3_h, w2_h), (w1, w3, w2), wsem)
    for c in weights:
        c.start()
    barrier(ids)
    gt, gy, gd, gx = [Gather(ids, ref, gsend.at[i], grecv.at[i]) for i, ref in enumerate((tab, yall, dall, xall))]
    for c, g in zip(local[:3], (gt, gy, gd)):
        c.wait()
    gt.start()
    gy.start()
    gt.relay_prim()
    gt.relay_rest()
    gt.finish()
    table_o[...] = jnp.transpose(tab[...])[0:32, :]
    build_onehot(table_o, 0, ids["me"], onehot, gate_col)
    gy.relay_prim()
    gd.start()
    gy.relay_rest()
    gy.finish()
    take_rows(onehot, yall, u)
    for e in range(LOCAL):
        weights[3 * e].wait()
        weights[3 * e + 1].wait()
    store_u = pltpu.make_async_copy(u, u_o, osem.at[0])
    store_u.start()
    forward = lambda e, carry: (forward_expert(e, u, w1, w3, a, b, hid), carry)[1]
    lax.fori_loop(0, 1, forward, 0)
    gd.relay_prim()
    local[3].wait()
    gx.start()
    lax.fori_loop(1, LOCAL, forward, 0)
    gd.relay_rest()
    gd.finish()
    take_rows(onehot, dall, z, gate_col)
    gx.relay_prim()
    for e in range(LOCAL):
        weights[3 * e + 2].wait()
    store_z = pltpu.make_async_copy(z, z_o, osem.at[1])
    store_h = pltpu.make_async_copy(hid, hid_o, osem.at[2])
    store_z.start()
    store_h.start()
    lax.fori_loop(0, LOCAL, lambda e, carry: (backward_expert(e, z, w1, w3, w2, a, b, dxr), carry)[1], 0)
    gx.relay_rest()
    store_a = pltpu.make_async_copy(a, da_o, osem.at[3])
    store_b = pltpu.make_async_copy(b, db_o, osem.at[4])
    store_a.start()
    store_b.start()
    gx.finish()
    store_x = pltpu.make_async_copy(xall, xall_o, osem.at[5])
    store_x.start()
    return_sums(ids, core, x, y, onehot, dxr, sums, inbox, xsend, xrecv, (s_me, s_x, s_y, s_d))
    for g in (gt, gy, gd, gx):
        g.drain()
    for c in (store_u, store_z, store_h, store_a, store_b, store_x):
        c.wait()


def layer_one_kernel(dy_h, r_me, r_x, r_y, r_d, table, xall_h, w1_h, w3_h, w2_h,
                     u_o, z_o, hid_o, da_o, db_o, dy1_o, s_me, s_x, s_y, s_d,
                     dall, xall, w1, w3, w2, onehot, gate_col, u, z, a, b, hid, dxr, sums, inbox,
                     lsem, wsem, osem, gsend, grecv, xsend, xrecv):
    ids, core, x, y = place()
    load_x = pltpu.make_async_copy(xall_h, xall, lsem.at[0])
    load_x.start()
    weights = fetch_weights((w1_h, w3_h, w2_h), (w1, w3, w2), wsem)
    for c in weights:
        c.start()
    dy1 = (dy_h[...].astype(F32) + ((r_me[...] + r_x[...]) + (r_y[...] + r_d[...]))).astype(BF16)
    dall[pl.ds(pl.multiple_of(ids["me"] * TOK, TOK), TOK), :] = dy1
    dy1_o[...] = dy1
    barrier(ids)
    gd = Gather(ids, dall, gsend, grecv)
    gd.start()
    build_onehot(table, 16, ids["me"], onehot, gate_col)
    load_x.wait()
    take_rows(onehot, xall, u)
    store_u = pltpu.make_async_copy(u, u_o, osem.at[0])
    store_u.start()
    for e in range(LOCAL):
        weights[3 * e].wait()
        weights[3 * e + 1].wait()
    forward = lambda e, carry: (forward_expert(e, u, w1, w3, a, b, hid), carry)[1]
    lax.fori_loop(0, 2, forward, 0)
    gd.relay_prim()
    lax.fori_loop(2, LOCAL, forward, 0)
    gd.relay_rest()
    gd.finish()
    take_rows(onehot, dall, z, gate_col)
    for e in range(LOCAL):
        weights[3 * e + 2].wait()
    store_z = pltpu.make_async_copy(z, z_o, osem.at[1])
    store_h = pltpu.make_async_copy(hid, hid_o, osem.at[2])
    store_z.start()
    store_h.start()
    lax.fori_loop(0, LOCAL, lambda e, carry: (backward_expert(e, z, w1, w3, w2, a, b, dxr), carry)[1], 0)
    store_a = pltpu.make_async_copy(a, da_o, osem.at[3])
    store_b = pltpu.make_async_copy(b, db_o, osem.at[4])
    store_a.start()
    store_b.start()
    return_sums(ids, core, x, y, onehot, dxr, sums, inbox, xsend, xrecv, (s_me, s_x, s_y, s_d))
    gd.drain()
    for c in (store_u, store_z, store_h, store_a, store_b):
        c.wait()


HBM_SPEC = pl.BlockSpec(memory_space=pl.ANY)
VMEM_SPEC = pl.BlockSpec(memory_space=pltpu.VMEM)


def compute_scratch():
    return [
        pltpu.VMEM((LOCAL, D, F), BF16), pltpu.VMEM((LOCAL, D, F), BF16), pltpu.VMEM((LOCAL, F, D), BF16),
        pltpu.VMEM((2, LOCAL * HALF_ROWS, 256), BF16), pltpu.VMEM((2, LOCAL * HALF_ROWS, 128), F32),
        pltpu.VMEM((LOCAL, ROWS, D), BF16), pltpu.VMEM((LOCAL, ROWS, D), BF16),
        pltpu.VMEM((LOCAL, ROWS, F), BF16), pltpu.VMEM((LOCAL, ROWS, F), BF16), pltpu.VMEM((LOCAL, ROWS, F), BF16),
        pltpu.VMEM((2, LOCAL * HALF_ROWS, D), BF16), pltpu.VMEM((8 * TOK, D), F32), pltpu.VMEM((4, TOK, D), F32),
    ]


ROW_OUTS = [jax.ShapeDtypeStruct((LOCAL, ROWS, D), BF16)] * 2 + [jax.ShapeDtypeStruct((LOCAL, ROWS, F), BF16)] * 3
SUM_OUTS = [jax.ShapeDtypeStruct((TOK, D), F32)] * 4
DMA = pltpu.SemaphoreType.DMA


def layer_two(tab, y_mid, dy_out, x_tokens, w1, w3, w2):
    all_tok = pltpu.VMEM((8 * TOK, D), BF16)
    return pl.pallas_call(
        layer_two_kernel, name="layer_two",
        out_shape=ROW_OUTS + [jax.ShapeDtypeStruct((8 * TOK, D), BF16), jax.ShapeDtypeStruct((32, 8 * TOK), F32)] + SUM_OUTS,
        in_specs=[HBM_SPEC] * 7, out_specs=[HBM_SPEC] * 6 + [VMEM_SPEC] * 5,
        scratch_shapes=[pltpu.VMEM((8 * TOK, 128), F32), all_tok, all_tok, all_tok] + compute_scratch()
        + [DMA((4,)), DMA((3, LOCAL)), DMA((6,)), DMA((4, 7)), DMA((4, 7)), DMA((4,)), DMA((4,))],
        compiler_params=pltpu.CompilerParams(collective_id=0, has_side_effects=True, vmem_limit_bytes=60 * 2**20),
        cost_estimate=pl.CostEstimate(flops=16 * 10**9, bytes_accessed=36 * 2**20, transcendentals=0),
    )(tab, y_mid, dy_out, x_tokens, w1, w3, w2)


def layer_one(dy_out, returned, table, xall, w1, w3, w2):
    all_tok = pltpu.VMEM((8 * TOK, D), BF16)
    return pl.pallas_call(
        layer_one_kernel, name="layer_one",
        out_shape=ROW_OUTS + [jax.ShapeDtypeStruct((TOK, D), BF16)] + SUM_OUTS,
        in_specs=[VMEM_SPEC] * 6 + [HBM_SPEC] * 4, out_specs=[HBM_SPEC] * 5 + [VMEM_SPEC] * 5,
        scratch_shapes=[all_tok, all_tok] + compute_scratch()
        + [DMA((1,)), DMA((3, LOCAL)), DMA((5,)), DMA((7,)), DMA((7,)), DMA((4,)), DMA((4,))],
        compiler_params=pltpu.CompilerParams(collective_id=1, has_side_effects=True, vmem_limit_bytes=60 * 2**20),
        cost_estimate=pl.CostEstimate(flops=16 * 10**9, bytes_accessed=36 * 2**20, transcendentals=0),
    )(dy_out, *returned, table, xall, w1, w3, w2)


PARTS = 4


def weight_grad_kernel(u, da, db, hid, z, dw1, dw3, dw2):
    dw1[0] = lax.dot_general(u[0], da[0], TRANS_A, preferred_element_type=F32)
    dw3[0] = lax.dot_general(u[0], db[0], TRANS_A, preferred_element_type=F32)
    dw2[0] = lax.dot_general(hid[0], z[0], TRANS_A, preferred_element_type=F32)


def weight_grads(u, z, hid, da, db):
    whole = lambda cols: pl.BlockSpec((1, ROWS, cols), lambda e, p: (e, 0, 0))
    piece = lambda cols: pl.BlockSpec((1, ROWS, cols // PARTS), lambda e, p: (e, 0, p))
    out_rows = lambda rows, cols: pl.BlockSpec((1, rows // PARTS, cols), lambda e, p: (e, p, 0))
    return pl.pallas_call(
        weight_grad_kernel, name="weight_grads", grid=(LOCAL, PARTS),
        in_specs=[piece(D), whole(F), whole(F), piece(F), whole(D)],
        out_specs=[out_rows(D, F), out_rows(D, F), out_rows(F, D)],
        out_shape=[jax.ShapeDtypeStruct((LOCAL, D, F), F32)] * 2 + [jax.ShapeDtypeStruct((LOCAL, F, D), F32)],
        compiler_params=pltpu.CompilerParams(vmem_limit_bytes=32 * 2**20),
        cost_estimate=pl.CostEstimate(flops=18 * 10**9, bytes_accessed=56 * 2**20, transcendentals=0),
    )(u, da, db, hid, z)


def exchange_sums(sums):
    swap = lambda mask: [(i, i ^ mask) for i in range(8)]
    return (sums[0],) + tuple(lax.ppermute(sums[k], "expert", swap(mask)) for k, mask in ((1, 2), (2, 4), (3, 6)))


def routing_keys(experts, slots, gates):
    source = lax.axis_index("expert") % 4
    keys = jnp.where(slots >= 0, experts * HALF_ROWS + source * CAP + slots, -1)
    return [keys.astype(F32), gates]


def solution(mesh):
    tok_spec = P(("data", "expert"), None)
    weight_spec = P("expert", None, None)
    grad_spec = P(("data", "expert"), None, None)

    def local_step(x_tokens, y_mid, dy_out, experts_one, gates_one, slots_one, experts_two, gates_two, slots_two, w_gate_one, w_up_one, w_down_one, w_gate_two, w_up_two, w_down_two):
        parts = routing_keys(experts_two, slots_two, gates_two) + routing_keys(experts_one, slots_one, gates_one)
        tab = jnp.concatenate(parts + [jnp.zeros((TOK, 96), F32)], axis=1)
        *rows_two, xall, table, s0, s1, s2, s3 = layer_two(tab, y_mid, dy_out, x_tokens, w_gate_two, w_up_two, w_down_two)
        returned = exchange_sums((s0, s1, s2, s3))
        grads_two = weight_grads(*rows_two)
        *rows_one, dy_mid, s0, s1, s2, s3 = layer_one(dy_out, returned, table, xall, w_gate_one, w_up_one, w_down_one)
        r = exchange_sums((s0, s1, s2, s3))
        grads_one = weight_grads(*rows_one)
        dx_tokens = (dy_mid.astype(F32) + ((r[0] + r[1]) + (r[2] + r[3]))).astype(BF16)
        return (dx_tokens, *grads_one, *grads_two)

    return jax.shard_map(local_step, mesh=mesh, in_specs=(tok_spec,) * 9 + (weight_spec,) * 6, out_specs=(tok_spec,) + (grad_spec,) * 6, check_vma=False)
```

time: 327 us -> 153 us (0.47); the launches traced: 322 us -> 152 us
  waiting for transfers between devices: 143 us -> 0.02 us
  matrix products: 123 us -> 0 us
  Pallas kernels: 0 us -> 122 us
  local copies, waits for them, and re-layouts: 33.4 us -> 19.7 us
  starting transfers between devices: 20.3 us -> 7.01 us
    all_to_all x6 -> x0, waiting for transfers between devices: 143 us -> none  [the longest x2 70.9 us: layer_backward(): lax.all_to_all(dx_rows, 'expert', 1, 0, tiled=True)]
    dot_general x22 -> x0, matrix products: 123 us -> none  [the longest x2 17.6 us: expert_grads(): jnp.einsum('erd,erf->edf', x_rows, d_gate, preferred_element_type=jnp.flo...]
    pallas_call x0 -> x4, Pallas kernels: none -> 122 us  [the longest x1 51.4 us: layer_two(): pl.pallas_call(layer_two_kernel, name='layer_two', out_shape=ROW_OUTS + [...]
    all_to_all x6 -> x0, starting transfers between devices: 20.3 us -> none  [the longest x2 7.48 us: layer_backward(): lax.all_to_all(z_send.reshape(n_experts, capacity, model_dim), 'expert',...]
    all_to_all x6 -> x0, local copies, waits for them, and re-layouts: 17.1 us -> none  [the longest x2 6.99 us: layer_backward(): lax.all_to_all(dx_rows, 'expert', 1, 0, tiled=True)]
    unnamed x68 -> x34, local copies, waits for them, and re-layouts: 3.79 us -> 18.6 us
    convert_element_type x2 -> x0, local copies, waits for them, and re-layouts: 11.5 us -> none  [expert_grads(): (jnp.einsum('erf,edf->erd', d_gate, w_gate, preferred_element_type=jnp.fl...]
    ppermute x0 -> x6, starting transfers between devices: none -> 7.01 us  [exchange_sums(): lax.ppermute(sums[k], 'expert', swap(mask))]
  transfers between devices with their start and end apart: 6 -> 6, of which waited for: 6 -> 0; matrix products, arithmetic and copies ran while one was open for 34% -> 0% of each run, Pallas kernels for 0% -> 25%
where the time goes in v1:
time: 153 us; the launch traced here: 152 us
  Pallas kernels  122 us (80%)
  local copies, waits for them, and re-layouts  19.7 us (13%)
  starting transfers between devices  7.01 us (5%)
  other arithmetic  2.89 us (2%)
    pallas_call x1, Pallas kernels, layer_two(): pl.pallas_call(layer_two_kernel, name='layer_two', out_shape=ROW_OUTS + [...  51.4 us
    pallas_call x2, Pallas kernels, weight_grads(): pl.pallas_call(weight_grad_kernel, name='weight_grads', grid=(LOCAL, PART...  37.4 us
    pallas_call x1, Pallas kernels, layer_one(): pl.pallas_call(layer_one_kernel, name='layer_one', out_shape=ROW_OUTS + [...  32.8 us
    unnamed x34, local copies, waits for them, and re-layouts  18.6 us
    ppermute x6, starting transfers between devices, exchange_sums(): lax.ppermute(sums[k], 'expert', swap(mask))  7.01 us
  transfers between devices with their start and end apart: 6, of which 0 were waited for; matrix products, arithmetic and copies ran while one was open for 0% of the time, Pallas kernels for 25%

profile of v1, /device:TPU:0, one launch (start us, length us, event | category | flops | bytes accessed | tf_op | source)
XLA Modules:
  0.0 152.0 jit_solution(497404352695163652)
XLA Ops:
  0.6 0.7 broadcast_compare_fusion
  1.3 0.8 copy.40
  2.1 0.7 broadcast_compare_fusion.1
  2.8 0.8 copy.37
  3.6 0.1 copy.38
  3.7 0.1 copy.41
  3.8 0.7 multiply_add_fusion
  4.5 0.1 copy.39
  4.6 0.1 copy.36
  4.7 0.8 copy.43
  5.4 0.8 copy.42
  6.2 0.7 concatenate.3.tab_h
  7.0 51.4 %layer_two.1 = (bf16[5,192,1536]{2,1,0:T(8,128)(2,1)}, bf16[5,192,1536]{2,1,0:T(8,128)(2,1)}, bf16[5,192,512]{2,1,0:T(8,128)(2,1)}, bf16[5,192,512]{2,1,0:T(8,12...) custom-call(f32[64,128]{1,0:T(8,128)} %concatenate.3.tab_h, ...), custom_call_target="tpu_custom_call" | custom-call | flops 16000000000 | bytes 37748736 | tf_op jit(solution)/shard_map/layer_two/pallas_call | solution.py:313
  58.4 0.0 collective-permute-start
  58.4 2.1 %collective-permute-start.1 = (f32[64,1536]{1,0:T(8,128)}, f32[64,1536]{1,0:T(8,128)S(1)}, u32[]{:S(2)}, u32[]{:S(2)}) collective-permute-start(f32[64,1536]{1,0:T(8,128)} %get-tuple-element.36), channel_id=1, source_target_pairs={{0,4},{1,5},{2,6},{3,7},{4,0},{5,1},{6,2},{7,3}} | collective-permute-start | bytes 1179656 | tf_op jit(solution)/shard_map/ppermute | solution.py:362
  60.5 1.4 collective-permute-start.2
  61.9 0.0 copy-start.2
  61.9 1.8 %copy-done.2 = bf16[5,192,1536]{2,1,0:T(8,128)(2,1)S(1)} copy-done((bf16[5,192,1536]{2,1,0:T(8,128)(2,1)S(1)}, bf16[5,192,1536]{2,1,0:T(8,128)(2,1)}, u32[]{:S(2)}) %copy-start.2) | copy-done | bytes 2949144
  63.7 0.0 copy-start.3
  63.7 1.8 %copy-done.3 = bf16[5,192,1536]{2,1,0:T(8,128)(2,1)S(1)} copy-done((bf16[5,192,1536]{2,1,0:T(8,128)(2,1)S(1)}, bf16[5,192,1536]{2,1,0:T(8,128)(2,1)}, u32[]{:S(2)}) %copy-start.3) | copy-done | bytes 2949144
  65.5 1.2 copy-done.7
  66.7 1.2 copy-done.8
  67.9 1.2 copy-done.9
  69.1 18.7 %weight_grads.3 = (f32[5,1536,512]{2,1,0:T(8,128)}, f32[5,1536,512]{2,1,0:T(8,128)}, f32[5,512,1536]{2,1,0:T(8,128)}) custom-call(bf16[5,192,1536]{2,1,0:T(8,128)(2,1)S(1)} %copy-done.2, bf16[5,192,512]{2,1,0:T(8,128)(2,1)S(1)} %copy-done.8, bf16[5,192,512]{2,1,0:T(8,128)(2,1)S(1)} %copy-done.9, bf16[5,192,512]{2,1,0:T(8,128)(2,1)S(1)} %copy-done.7, ...), custom_call_target="tpu_custom_call" | custom-call | flops 17999998976 | bytes 58720256 | tf_op jit(solution)/shard_map/weight_grads/pallas_call | solution.py:350
  87.9 0.0 collective-permute-done.r_x
  87.9 0.0 collective-permute-done.1.r_y
  87.9 0.0 copy-start.13
  87.9 0.0 collective-permute-done.2.r_d
  87.9 0.0 copy-start.14
  87.9 0.7 copy-done.12
  88.6 0.1 copy-done.13
  88.7 0.1 copy-done.14
  88.9 32.8 %layer_one.1 = (bf16[5,192,1536]{2,1,0:T(8,128)(2,1)}, bf16[5,192,1536]{2,1,0:T(8,128)(2,1)}, bf16[5,192,512]{2,1,0:T(8,128)(2,1)}, bf16[5,192,512]{2,1,0:T(8,12...) custom-call(bf16[64,1536]{1,0:T(8,128)(2,1)} %dy_h.3, ...), custom_call_target="tpu_custom_call" | custom-call | flops 16000000000 | bytes 37748736 | tf_op jit(solution)/shard_map/layer_one/pallas_call | solution.py:326
  121.7 1.5 collective-permute-start.3
  123.2 0.0 collective-permute-start.4
  123.2 2.0 %collective-permute-start.5 = (f32[64,1536]{1,0:T(8,128)}, f32[64,1536]{1,0:T(8,128)S(1)}, u32[]{:S(2)}, u32[]{:S(2)}) collective-permute-start(f32[64,1536]{1,0:T(8,128)} %get-tuple-element.44), channel_id=1, source_target_pairs={{0,6},{1,7},{2,4},{3,5},{4,2},{5,3},{6,0},{7,1}} | collective-permute-start | bytes 1179656 | tf_op jit(solution)/shard_map/ppermute | solution.py:362
  125.2 1.8 %copy-done = bf16[5,192,1536]{2,1,0:T(8,128)(2,1)S(1)} copy-done((bf16[5,192,1536]{2,1,0:T(8,128)(2,1)S(1)}, bf16[5,192,1536]{2,1,0:T(8,128)(2,1)}, u32[]{:S(2)}) %copy-start) | copy-done | bytes 2949144
  127.0 1.8 %copy-done.1 = bf16[5,192,1536]{2,1,0:T(8,128)(2,1)S(1)} copy-done((bf16[5,192,1536]{2,1,0:T(8,128)(2,1)S(1)}, bf16[5,192,1536]{2,1,0:T(8,128)(2,1)}, u32[]{:S(2)}) %copy-start.1) | copy-done | bytes 2949144
  128.9 1.2 copy-done.4
  130.1 1.2 copy-done.5
  131.3 1.2 copy-done.6
  132.5 18.7 %weight_grads.2 = (f32[5,1536,512]{2,1,0:T(8,128)}, f32[5,1536,512]{2,1,0:T(8,128)}, f32[5,512,1536]{2,1,0:T(8,128)}) custom-call(bf16[5,192,1536]{2,1,0:T(8,128)(2,1)S(1)} %copy-done, bf16[5,192,512]{2,1,0:T(8,128)(2,1)S(1)} %copy-done.5, bf16[5,192,512]{2,1,0:T(8,128)(2,1)S(1)} %copy-done.6, bf16[5,192,512]{2,1,0:T(8,128)(2,1)S(1)} %copy-done.4, ...), custom_call_target="tpu_custom_call" | custom-call | flops 17999998976 | bytes 58720256 | tf_op jit(solution)/shard_map/weight_grads/pallas_call | solution.py:350
  151.2 0.0 collective-permute-done.3
  151.2 0.0 collective-permute-done.4
  151.2 0.0 collective-permute-done.5
  151.2 0.0 copy-done.10
  151.2 0.0 copy-done.11
  151.2 0.8 add_convert_fusion
  (14 shorter events, 0.0 us)
Async XLA Ops:
  58.4 29.5 %collective-permute-start = (f32[64,1536]{1,0:T(8,128)}, f32[64,1536]{1,0:T(8,128)S(1)}, u32[]{:S(2)}, u32[]{:S(2)}) collective-permute-start(f32[64,1536]{1,0:T(8,128)} %get-tuple-element.35), channel_id=1, source_target_pairs={{0,2},{1,3},{2,0},{3,1},{4,6},{5,7},{6,4},{7,5}} | collective-permute-start | bytes 1179656 | tf_op jit(solution)/shard_map/ppermute | solution.py:362
  58.4 29.5 %collective-permute-start.1 = (f32[64,1536]{1,0:T(8,128)}, f32[64,1536]{1,0:T(8,128)S(1)}, u32[]{:S(2)}, u32[]{:S(2)}) collective-permute-start(f32[64,1536]{1,0:T(8,128)} %get-tuple-element.36), channel_id=1, source_target_pairs={{0,4},{1,5},{2,6},{3,7},{4,0},{5,1},{6,2},{7,3}} | collective-permute-start | bytes 1179656 | tf_op jit(solution)/shard_map/ppermute | solution.py:362
  60.5 27.4 %collective-permute-start.2 = (f32[64,1536]{1,0:T(8,128)}, f32[64,1536]{1,0:T(8,128)S(1)}, u32[]{:S(2)}, u32[]{:S(2)}) collective-permute-start(f32[64,1536]{1,0:T(8,128)} %get-tuple-element.37), channel_id=1, source_target_pairs={{0,6},{1,7},{2,4},{3,5},{4,2},{5,3},{6,0},{7,1}} | collective-permute-start | bytes 1179656 | tf_op jit(solution)/shard_map/ppermute | solution.py:362
  61.9 1.8 %copy-start.2 = (bf16[5,192,1536]{2,1,0:T(8,128)(2,1)S(1)}, bf16[5,192,1536]{2,1,0:T(8,128)(2,1)}, u32[]{:S(2)}) copy-start(bf16[5,192,1536]{2,1,0:T(8,128)(2,1)} %get-tuple-element.53.u) | copy-start | bytes 8847364
  63.7 1.8 %copy-start.3 = (bf16[5,192,1536]{2,1,0:T(8,128)(2,1)S(1)}, bf16[5,192,1536]{2,1,0:T(8,128)(2,1)}, u32[]{:S(2)}) copy-start(bf16[5,192,1536]{2,1,0:T(8,128)(2,1)} %get-tuple-element.57.z) | copy-start | bytes 8847364
  65.5 1.2 copy-start.7
  66.7 1.2 copy-start.8
  67.9 1.2 copy-start.9
  87.9 0.7 copy-start.12
  87.9 0.9 copy-start.13
  87.9 1.0 copy-start.14
  121.7 29.5 %collective-permute-start.3 = (f32[64,1536]{1,0:T(8,128)}, f32[64,1536]{1,0:T(8,128)S(1)}, u32[]{:S(2)}, u32[]{:S(2)}) collective-permute-start(f32[64,1536]{1,0:T(8,128)} %get-tuple-element.42), channel_id=1, source_target_pairs={{0,2},{1,3},{2,0},{3,1},{4,6},{5,7},{6,4},{7,5}} | collective-permute-start | bytes 1179656 | tf_op jit(solution)/shard_map/ppermute | solution.py:362
  123.2 28.0 %collective-permute-start.4 = (f32[64,1536]{1,0:T(8,128)}, f32[64,1536]{1,0:T(8,128)S(1)}, u32[]{:S(2)}, u32[]{:S(2)}) collective-permute-start(f32[64,1536]{1,0:T(8,128)} %get-tuple-element.43), channel_id=1, source_target_pairs={{0,4},{1,5},{2,6},{3,7},{4,0},{5,1},{6,2},{7,3}} | collective-permute-start | bytes 1179656 | tf_op jit(solution)/shard_map/ppermute | solution.py:362
  123.2 28.0 %collective-permute-start.5 = (f32[64,1536]{1,0:T(8,128)}, f32[64,1536]{1,0:T(8,128)S(1)}, u32[]{:S(2)}, u32[]{:S(2)}) collective-permute-start(f32[64,1536]{1,0:T(8,128)} %get-tuple-element.44), channel_id=1, source_target_pairs={{0,6},{1,7},{2,4},{3,5},{4,2},{5,3},{6,0},{7,1}} | collective-permute-start | bytes 1179656 | tf_op jit(solution)/shard_map/ppermute | solution.py:362
  125.2 1.8 %copy-start = (bf16[5,192,1536]{2,1,0:T(8,128)(2,1)S(1)}, bf16[5,192,1536]{2,1,0:T(8,128)(2,1)}, u32[]{:S(2)}) copy-start(bf16[5,192,1536]{2,1,0:T(8,128)(2,1)} %get-tuple-element.45.u) | copy-start | bytes 8847364
  127.0 1.8 %copy-start.1 = (bf16[5,192,1536]{2,1,0:T(8,128)(2,1)S(1)}, bf16[5,192,1536]{2,1,0:T(8,128)(2,1)}, u32[]{:S(2)}) copy-start(bf16[5,192,1536]{2,1,0:T(8,128)(2,1)} %get-tuple-element.49.z) | copy-start | bytes 8847364
  128.9 1.2 copy-start.4
  130.1 1.2 copy-start.5
  131.3 1.2 copy-start.6
  132.5 18.7 %copy-start.10 = (f32[64,1536]{1,0:T(8,128)S(1)}, f32[64,1536]{1,0:T(8,128)}, u32[]{:S(2)}) copy-start(f32[64,1536]{1,0:T(8,128)} %get-tuple-element.41) | copy-start | bytes 1179652
  132.5 18.7 %copy-start.11 = (bf16[64,1536]{1,0:T(8,128)(2,1)S(1)}, bf16[64,1536]{1,0:T(8,128)(2,1)}, u32[]{:S(2)}) copy-start(bf16[64,1536]{1,0:T(8,128)(2,1)} %get-tuple-element.40) | copy-start | bytes 589828

commit v2 on v1

v2 whole, which is shorter than its diff:
```python
import functools
import jax
import jax.numpy as jnp
from jax import lax
from jax.experimental import pallas as pl
from jax.experimental.pallas import tpu as pltpu
from jax.sharding import PartitionSpec as P

MESH = pl.DeviceIdType.MESH
F32 = jnp.float32
BF16 = jnp.bfloat16
CAP = 24
LOCAL = 5
D = 1536
F = 512
TOK = 64
HALF_ROWS = 4 * CAP
ROWS = 8 * CAP
STEP = 512


def place():
    me = lax.axis_index("expert")
    core, x, y = me % 2, (me // 2) % 2, me // 4
    ident = lambda xx, yy, cc: 4 * yy + 2 * xx + cc
    ids = {
        "me": me,
        "partner": ident(x, y, 1 - core),
        "x": ident(1 - x, y, core),
        "y": ident(x, 1 - y, core),
        "diag": ident(1 - x, 1 - y, core),
        "prim": ident(x + (1 - core) * (1 - 2 * x), y + core * (1 - 2 * y), core),
        "sec": ident(x + core * (1 - 2 * x), y + (1 - core) * (1 - 2 * y), core),
        "p_prim": ident(x + core * (1 - 2 * x), y + (1 - core) * (1 - 2 * y), 1 - core),
        "p_sec": ident(x + (1 - core) * (1 - 2 * x), y + core * (1 - 2 * y), 1 - core),
        "p_diag": ident(1 - x, 1 - y, 1 - core),
    }
    return ids, core, x, y


def barrier(ids):
    sem = pltpu.get_barrier_semaphore()
    for peer in ("partner", "x", "y"):
        pl.semaphore_signal(sem, inc=1, device_id={"expert": ids[peer]}, device_id_type=MESH)
    pl.semaphore_wait(sem, 3)


def block(ref, ident):
    return ref.at[pl.ds(pl.multiple_of(ident * TOK, TOK), TOK)]


class Gather:
    ROUTES = (("me", "partner"), ("me", "prim"), ("me", "sec"), ("prim", "sec"), ("prim", "partner"), ("sec", "partner"), ("diag", "partner"))
    ARRIVE = ("partner", "prim", "sec", "diag", "p_prim", "p_sec", "p_diag")

    def __init__(self, ids, ref, send, recv, pieces):
        self.ids, self.ref, self.send, self.recv, self.pieces = ids, ref, send, recv, pieces

    def part(self, ident, i):
        if self.pieces == 0:
            return self.ref.at[ident]
        size = TOK // self.pieces
        return self.ref.at[pl.ds(pl.multiple_of(ident * TOK + i * size, size), size)]

    def copy(self, k, i, what=None, where=None):
        what, where = what or self.ROUTES[k][0], where or self.ROUTES[k][1]
        part = self.part(self.ids[what], i)
        return pltpu.make_async_remote_copy(src_ref=part, dst_ref=part, send_sem=self.send.at[i, k], recv_sem=self.recv.at[i, k], device_id={"expert": self.ids[where]}, device_id_type=MESH)

    def arrived(self, k, i):
        self.copy(k, i, self.ARRIVE[k], "partner").wait_recv()

    def every(self):
        return range(max(self.pieces, 1))

    def start(self, k):
        for i in self.every():
            self.copy(k, i).start()

    def relay_prim(self, i):
        self.arrived(1, i)
        self.copy(3, i).start()
        self.copy(4, i).start()

    def relay_rest(self, i):
        self.arrived(2, i)
        self.copy(5, i).start()
        self.arrived(3, i)
        self.copy(6, i).start()

    def finish(self):
        for i in self.every():
            for k in (0, 4, 5, 6):
                self.arrived(k, i)

    def drain(self):
        for i in self.every():
            for k in range(7):
                self.copy(k, i).wait_send()


PARTNER, PRIM, SEC = 0, 1, 2


def fill_table(routing, me, out):
    out[...] = jnp.zeros((32, 128), F32)
    for layer in range(2):
        experts, slots, gates = (routing[3 * layer + k] for k in range(3))
        keys = jnp.where(slots[...] >= 0, experts[...] * HALF_ROWS + (me % 4) * CAP + slots[...], -1)
        out[16 * layer : 16 * layer + 8, 0:TOK] = keys.astype(F32)
        out[16 * layer + 8 : 16 * layer + 16, 0:TOK] = gates[...]


def join_table(tab, table):
    low = lax.broadcasted_iota(jnp.int32, (32, 128), 1) < TOK
    for p in range(4):
        table[:, p * 128 : (p + 1) * 128] = jnp.where(low, tab[2 * p], pltpu.roll(tab[2 * p + 1], TOK, 1))


def build_onehot(table, base, me, onehot, gate_col):
    for h in range(2):
        cols = slice(h * 256, (h + 1) * 256)
        keys = [table[base + j : base + j + 1, cols] for j in range(8)]
        gates = [table[base + 8 + j : base + 9 + j, cols] for j in range(8)]
        for e in range(LOCAL):
            row = (lax.broadcasted_iota(jnp.int32, (HALF_ROWS, 256), 0) + (e + me * LOCAL) * HALF_ROWS).astype(F32)
            gate = jnp.zeros((HALF_ROWS, 256), F32)
            hit = jnp.zeros((HALF_ROWS, 256), F32)
            for j in range(8):
                match = row == keys[j]
                gate = jnp.where(match, gates[j], gate)
                hit = jnp.where(match, 1.0, hit)
            onehot[h, e * HALF_ROWS : (e + 1) * HALF_ROWS, :] = hit.astype(BF16)
            gate_col[h, e * HALF_ROWS : (e + 1) * HALF_ROWS, :] = jnp.broadcast_to(jnp.sum(gate, axis=1, keepdims=True), (HALF_ROWS, 128))


def take_rows(onehot, tokens, rows, gate_col=None):
    for h in range(2):
        for n in range(D // STEP):
            cols = slice(n * STEP, (n + 1) * STEP)
            out = jnp.dot(onehot[h], tokens[h * 256 : (h + 1) * 256, cols], preferred_element_type=F32)
            if gate_col is not None:
                out = out * gate_col[h, :, 0:1]
            out = out.astype(BF16)
            for e in range(LOCAL):
                rows[e, h * HALF_ROWS : (h + 1) * HALF_ROWS, cols] = out[e * HALF_ROWS : (e + 1) * HALF_ROWS]


def forward_expert(e, u, w1, w3, a, b, hid):
    act = jnp.dot(u[e], w1[e], preferred_element_type=F32).astype(BF16)
    up = jnp.dot(u[e], w3[e], preferred_element_type=F32).astype(BF16)
    a[e] = act
    b[e] = up
    wide = act.astype(F32)
    hid[e] = (wide * jax.nn.sigmoid(wide) * up.astype(F32)).astype(BF16)


TRANS_B = (((1,), (1,)), ((), ()))
TRANS_A = (((0,), (0,)), ((), ()))


def hidden_grads(e, z, w2, a, b):
    dh = lax.dot_general(z[e], w2[e], TRANS_B, preferred_element_type=F32)
    act = a[e].astype(F32)
    up = b[e].astype(F32)
    sig = jax.nn.sigmoid(act)
    a[e] = (dh * up * sig * (1.0 + act * (1.0 - sig))).astype(BF16)
    b[e] = (dh * (act * sig)).astype(BF16)


def row_grads(e, cols, w1, w3, a, b, dxr):
    dx = lax.dot_general(a[e], w1[e, cols, :], TRANS_B, preferred_element_type=F32) + lax.dot_general(b[e], w3[e, cols, :], TRANS_B, preferred_element_type=F32)
    dx = dx.astype(BF16)
    for h in range(2):
        dxr[h, e * HALF_ROWS : (e + 1) * HALF_ROWS, cols] = dx[h * HALF_ROWS : (h + 1) * HALF_ROWS]


def return_sums(ids, core, x, y, onehot, w1, w3, a, b, dxr, sums, inbox, send, recv, ssem, outs, between):
    def exchange(n, yy, xx):
        theirs = 4 * yy + 2 * xx + (1 - core)
        cols = pl.ds(n * STEP, STEP)
        src = sums.at[pl.ds(pl.multiple_of(theirs * TOK, TOK), TOK), cols]
        return pltpu.make_async_remote_copy(src_ref=src, dst_ref=inbox.at[2 * yy + xx, :, cols], send_sem=send.at[n, 2 * yy + xx], recv_sem=recv.at[n, 2 * yy + xx], device_id={"expert": ids["partner"]}, device_id_type=MESH)

    def store(n, name, xx, yy, out, k):
        cols = pl.ds(n * STEP, STEP)
        return pltpu.make_async_copy(inbox.at[2 * yy + xx, :, cols], out.at[:, cols], ssem.at[n, k])

    blocks = (("me", x, y, outs[0], 0), ("x", 1 - x, y, outs[1], 1), ("y", x, 1 - y, outs[2], 2), ("diag", 1 - x, 1 - y, outs[3], 3))

    def collect(n):
        for k in range(4):
            exchange(n, k // 2, k % 2).wait_recv()
        cols = slice(n * STEP, (n + 1) * STEP)
        for name, xx, yy, out, k in blocks:
            inbox[2 * yy + xx, :, cols] = inbox[2 * yy + xx, :, cols] + sums[pl.ds(pl.multiple_of(ids[name] * TOK, TOK), TOK), cols]
            store(n, name, xx, yy, out, k).start()

    for n in range(D // STEP):
        cols = slice(n * STEP, (n + 1) * STEP)
        for e in range(LOCAL):
            row_grads(e, cols, w1, w3, a, b, dxr)
        for h in range(2):
            sums[h * 256 : (h + 1) * 256, cols] = lax.dot_general(onehot[h], dxr[h, :, cols], TRANS_A, preferred_element_type=F32)
        for k in range(4):
            exchange(n, k // 2, k % 2).start()
        if n > 0:
            collect(n - 1)
        between(n)
    collect(D // STEP - 1)
    for n in range(D // STEP):
        for k in range(4):
            exchange(n, k // 2, k % 2).wait_send()
        for entry in blocks:
            store(n, *entry).wait()


class Weights:
    def __init__(self, hbm, vmem, sems):
        self.hbm, self.vmem, self.sems = hbm, vmem, sems

    def copy(self, k, e):
        return pltpu.make_async_copy(self.hbm[k].at[e], self.vmem[k].at[e], self.sems.at[k, e])

    def start(self, kinds, experts):
        for e in experts:
            for k in kinds:
                self.copy(k, e).start()

    def wait(self, kinds, e):
        for k in kinds:
            self.copy(k, e).wait()


def layer_two_kernel(*refs):
    routing_h, refs = refs[:6], refs[6:]
    (y_h, dy_h, x_h, w1_h, w3_h, w2_h,
     u_o, z_o, hid_o, da_o, db_o, xall_o, table_o, s_me, s_x, s_y, s_d) = refs[:17]
    routing, refs = refs[17:23], refs[23:]
    (tab, yall, dall, xall, w1, w3, w2, onehot, gate_col, u, z, a, b, hid, dxr, sums, inbox,
     lsem, wsem, osem, tsend, trecv, gsend, grecv, xsend, xrecv, ssem) = refs
    ids, core, x, y = place()
    small = [pltpu.make_async_copy(src, dst, lsem.at[3 + i]) for i, (src, dst) in enumerate(zip(routing_h, routing))]
    local = [pltpu.make_async_copy(src, block(dst, ids["me"]), lsem.at[i]) for i, (src, dst) in enumerate(((y_h, yall), (dy_h, dall), (x_h, xall)))]
    for c in small + local:
        c.start()
    for c in small:
        c.wait()
    fill_table(routing, ids["me"], tab.at[ids["me"]])
    for c in local:
        c.wait()
    weights = Weights((w1_h, w3_h, w2_h), (w1, w3, w2), wsem)
    weights.start((0, 1, 2), range(LOCAL))
    barrier(ids)
    gt = Gather(ids, tab, tsend, trecv, 0)
    gy, gd, gx = [Gather(ids, ref, gsend.at[i], grecv.at[i], 2) for i, ref in enumerate((yall, dall, xall))]
    for k in (PRIM, SEC, PARTNER):
        gt.start(k)
    for k in (PRIM, SEC, PARTNER):
        gy.start(k)
    for k in (PRIM, PARTNER):
        gd.start(k)
    gt.relay_prim(0)
    gy.relay_prim(0)
    gt.relay_rest(0)
    gt.finish()
    gy.relay_prim(1)
    gd.start(SEC)
    join_table(tab, table_o)
    build_onehot(table_o, 0, ids["me"], onehot, gate_col)
    gy.relay_rest(0)
    gy.relay_rest(1)
    gy.finish()
    take_rows(onehot, yall, u)
    store_u = pltpu.make_async_copy(u, u_o, osem.at[0])
    store_u.start()

    def forward(first, last):
        for e in range(first, last):
            weights.wait((0, 1), e)
            forward_expert(e, u, w1, w3, a, b, hid)

    forward(0, 1)
    gd.relay_prim(0)
    gd.relay_prim(1)
    for k in (PRIM, SEC, PARTNER):
        gx.start(k)
    forward(1, LOCAL)
    gd.relay_rest(0)
    gd.relay_rest(1)
    gd.finish()
    take_rows(onehot, dall, z, gate_col)
    gx.relay_prim(0)
    store_z = pltpu.make_async_copy(z, z_o, osem.at[1])
    store_h = pltpu.make_async_copy(hid, hid_o, osem.at[2])
    store_z.start()
    store_h.start()
    for e in range(LOCAL):
        weights.wait((2,), e)
        hidden_grads(e, z, w2, a, b)
    gx.relay_prim(1)
    store_a = pltpu.make_async_copy(a, da_o, osem.at[3])
    store_b = pltpu.make_async_copy(b, db_o, osem.at[4])
    store_a.start()
    store_b.start()
    store_x = pltpu.make_async_copy(xall, xall_o, osem.at[5])

    def between(n):
        if n == 0:
            gx.relay_rest(0)
            gx.relay_rest(1)
        if n == 1:
            gx.finish()
            store_x.start()

    return_sums(ids, core, x, y, onehot, w1, w3, a, b, dxr, sums, inbox, xsend, xrecv, ssem, (s_me, s_x, s_y, s_d), between)
    for g in (gt, gy, gd, gx):
        g.drain()
    for c in (store_u, store_z, store_h, store_a, store_b, store_x):
        c.wait()


def layer_one_kernel(dy_h, r_me, r_x, r_y, r_d, table, xall_h, w1_h, w3_h, w2_h,
                     u_o, z_o, hid_o, da_o, db_o, dy1_o, s_me, s_x, s_y, s_d,
                     dall, xall, w1, w3, w2, onehot, gate_col, u, z, a, b, hid, dxr, sums, inbox,
                     lsem, wsem, osem, gsend, grecv, xsend, xrecv, ssem):
    ids, core, x, y = place()
    load_x = pltpu.make_async_copy(xall_h, xall, lsem.at[0])
    load_x.start()
    weights = Weights((w1_h, w3_h, w2_h), (w1, w3, w2), wsem)
    dy1 = (dy_h[...].astype(F32) + ((r_me[...] + r_x[...]) + (r_y[...] + r_d[...]))).astype(BF16)
    dall[pl.ds(pl.multiple_of(ids["me"] * TOK, TOK), TOK), :] = dy1
    dy1_o[...] = dy1
    barrier(ids)
    gd = Gather(ids, dall, gsend, grecv, 2)
    for k in (PRIM, SEC, PARTNER):
        gd.start(k)
    load_x.wait()
    weights.start((0, 1), (0, 1))
    build_onehot(table, 16, ids["me"], onehot, gate_col)
    weights.start((0, 1), (2, 3, 4))
    take_rows(onehot, xall, u)
    weights.start((2,), range(LOCAL))
    store_u = pltpu.make_async_copy(u, u_o, osem.at[0])
    store_u.start()

    def forward(first, last):
        for e in range(first, last):
            weights.wait((0, 1), e)
            forward_expert(e, u, w1, w3, a, b, hid)

    forward(0, 1)
    gd.relay_prim(0)
    forward(1, 2)
    gd.relay_prim(1)
    forward(2, LOCAL)
    gd.relay_rest(0)
    gd.relay_rest(1)
    gd.finish()
    take_rows(onehot, dall, z, gate_col)
    store_z = pltpu.make_async_copy(z, z_o, osem.at[1])
    store_h = pltpu.make_async_copy(hid, hid_o, osem.at[2])
    store_z.start()
    store_h.start()
    for e in range(LOCAL):
        weights.wait((2,), e)
        hidden_grads(e, z, w2, a, b)
    store_a = pltpu.make_async_copy(a, da_o, osem.at[3])
    store_b = pltpu.make_async_copy(b, db_o, osem.at[4])
    store_a.start()
    store_b.start()
    return_sums(ids, core, x, y, onehot, w1, w3, a, b, dxr, sums, inbox, xsend, xrecv, ssem, (s_me, s_x, s_y, s_d), lambda n: None)
    gd.drain()
    for c in (store_u, store_z, store_h, store_a, store_b):
        c.wait()


HBM_SPEC = pl.BlockSpec(memory_space=pl.ANY)
VMEM_SPEC = pl.BlockSpec(memory_space=pltpu.VMEM)


def compute_scratch():
    return [
        pltpu.VMEM((LOCAL, D, F), BF16), pltpu.VMEM((LOCAL, D, F), BF16), pltpu.VMEM((LOCAL, F, D), BF16),
        pltpu.VMEM((2, LOCAL * HALF_ROWS, 256), BF16), pltpu.VMEM((2, LOCAL * HALF_ROWS, 128), F32),
        pltpu.VMEM((LOCAL, ROWS, D), BF16), pltpu.VMEM((LOCAL, ROWS, D), BF16),
        pltpu.VMEM((LOCAL, ROWS, F), BF16), pltpu.VMEM((LOCAL, ROWS, F), BF16), pltpu.VMEM((LOCAL, ROWS, F), BF16),
        pltpu.VMEM((2, LOCAL * HALF_ROWS, D), BF16), pltpu.VMEM((8 * TOK, D), F32), pltpu.VMEM((4, TOK, D), F32),
    ]


ROW_OUTS = [jax.ShapeDtypeStruct((LOCAL, ROWS, D), BF16)] * 2 + [jax.ShapeDtypeStruct((LOCAL, ROWS, F), BF16)] * 3
SUM_OUTS = [jax.ShapeDtypeStruct((TOK, D), F32)] * 4
DMA = pltpu.SemaphoreType.DMA


def layer_two(routing, y_mid, dy_out, x_tokens, w1, w3, w2):
    all_tok = pltpu.VMEM((8 * TOK, D), BF16)
    table_in = [pltpu.VMEM((8, TOK), t) for t in (jnp.int32, jnp.int32, F32)]
    return pl.pallas_call(
        layer_two_kernel, name="layer_two",
        out_shape=ROW_OUTS + [jax.ShapeDtypeStruct((8 * TOK, D), BF16), jax.ShapeDtypeStruct((32, 8 * TOK), F32)] + SUM_OUTS,
        in_specs=[HBM_SPEC] * 12, out_specs=[HBM_SPEC] * 6 + [VMEM_SPEC] + [HBM_SPEC] * 4,
        scratch_shapes=table_in * 2 + [pltpu.VMEM((8, 32, 128), F32), all_tok, all_tok, all_tok] + compute_scratch()
        + [DMA((9,)), DMA((3, LOCAL)), DMA((6,)), DMA((1, 7)), DMA((1, 7)), DMA((3, 2, 7)), DMA((3, 2, 7)), DMA((3, 4)), DMA((3, 4)), DMA((3, 4))],
        compiler_params=pltpu.CompilerParams(collective_id=0, has_side_effects=True, vmem_limit_bytes=56 * 2**20),
        cost_estimate=pl.CostEstimate(flops=16 * 10**9, bytes_accessed=36 * 2**20, transcendentals=0),
    )(*routing, y_mid, dy_out, x_tokens, w1, w3, w2)


def layer_one(dy_out, returned, table, xall, w1, w3, w2):
    all_tok = pltpu.VMEM((8 * TOK, D), BF16)
    return pl.pallas_call(
        layer_one_kernel, name="layer_one",
        out_shape=ROW_OUTS + [jax.ShapeDtypeStruct((TOK, D), BF16)] + SUM_OUTS,
        in_specs=[VMEM_SPEC] * 6 + [HBM_SPEC] * 4, out_specs=[HBM_SPEC] * 5 + [VMEM_SPEC] + [HBM_SPEC] * 4,
        scratch_shapes=[all_tok, all_tok] + compute_scratch()
        + [DMA((1,)), DMA((3, LOCAL)), DMA((5,)), DMA((2, 7)), DMA((2, 7)), DMA((3, 4)), DMA((3, 4)), DMA((3, 4))],
        compiler_params=pltpu.CompilerParams(collective_id=1, has_side_effects=True, vmem_limit_bytes=50 * 2**20),
        cost_estimate=pl.CostEstimate(flops=16 * 10**9, bytes_accessed=36 * 2**20, transcendentals=0),
    )(dy_out, *returned, table, xall, w1, w3, w2)


PARTS = 4


def weight_grad_kernel(u_h, z_h, hid_h, da_h, db_h, dw1_h, dw3_h, dw2_h, u, z, hid, da, db, ring1, ring3, ring2, isem, osem):
    def load(e):
        return [pltpu.make_async_copy(src.at[e], dst.at[e], isem.at[k, e]) for k, (src, dst) in enumerate(((u_h, u), (da_h, da), (db_h, db), (hid_h, hid), (z_h, z)))]

    for e in range(LOCAL):
        for c in load(e):
            c.start()

    def store(e, p):
        rows, cols = D // PARTS, F // PARTS
        return [pltpu.make_async_copy(ring1.at[p], dw1_h.at[e, pl.ds(p * rows, rows)], osem.at[0, p]),
                pltpu.make_async_copy(ring3.at[p], dw3_h.at[e, pl.ds(p * rows, rows)], osem.at[1, p]),
                pltpu.make_async_copy(ring2.at[p], dw2_h.at[e, pl.ds(p * cols, cols)], osem.at[2, p])]

    def expert(e, carry):
        for c in load(e):
            c.wait()
        for p in range(PARTS):
            rows, cols = slice(p * (D // PARTS), (p + 1) * (D // PARTS)), slice(p * (F // PARTS), (p + 1) * (F // PARTS))
            out = store(e, p)

            @pl.when(e > 0)
            def _():
                for c in out:
                    c.wait()

            ring1[p] = lax.dot_general(u[e, :, rows], da[e], TRANS_A, preferred_element_type=F32)
            out[0].start()
            ring3[p] = lax.dot_general(u[e, :, rows], db[e], TRANS_A, preferred_element_type=F32)
            out[1].start()
            ring2[p] = lax.dot_general(hid[e, :, cols], z[e], TRANS_A, preferred_element_type=F32)
            out[2].start()
        return carry

    lax.fori_loop(0, LOCAL, expert, 0)
    for p in range(PARTS):
        for c in store(LOCAL - 1, p):
            c.wait()


def weight_grads(u, z, hid, da, db):
    wide, narrow = pltpu.VMEM((LOCAL, ROWS, D), BF16), pltpu.VMEM((LOCAL, ROWS, F), BF16)
    ring = pltpu.VMEM((PARTS, D // PARTS, F), F32)
    return pl.pallas_call(
        weight_grad_kernel, name="weight_grads",
        in_specs=[HBM_SPEC] * 5, out_specs=[HBM_SPEC] * 3,
        out_shape=[jax.ShapeDtypeStruct((LOCAL, D, F), F32)] * 2 + [jax.ShapeDtypeStruct((LOCAL, F, D), F32)],
        scratch_shapes=[wide, wide, narrow, narrow, narrow, ring, ring, pltpu.VMEM((PARTS, F // PARTS, D), F32), DMA((5, LOCAL)), DMA((3, PARTS))],
        compiler_params=pltpu.CompilerParams(vmem_limit_bytes=60 * 2**20),
        cost_estimate=pl.CostEstimate(flops=18 * 10**9, bytes_accessed=56 * 2**20, transcendentals=0),
    )(u, z, hid, da, db)


def exchange_sums(sums):
    swap = lambda mask: [(i, i ^ mask) for i in range(8)]
    return (sums[0],) + tuple(lax.ppermute(sums[k], "expert", swap(mask)) for k, mask in ((1, 2), (2, 4), (3, 6)))


def solution(mesh):
    tok_spec = P(("data", "expert"), None)
    weight_spec = P("expert", None, None)
    grad_spec = P(("data", "expert"), None, None)

    def local_step(x_tokens, y_mid, dy_out, experts_one, gates_one, slots_one, experts_two, gates_two, slots_two, w_gate_one, w_up_one, w_down_one, w_gate_two, w_up_two, w_down_two):
        routing = [r.T for r in (experts_two, slots_two, gates_two, experts_one, slots_one, gates_one)]
        *rows_two, xall, table, s0, s1, s2, s3 = layer_two(routing, y_mid, dy_out, x_tokens, w_gate_two, w_up_two, w_down_two)
        returned = exchange_sums((s0, s1, s2, s3))
        grads_two = weight_grads(*rows_two)
        *rows_one, dy_mid, s0, s1, s2, s3 = layer_one(dy_out, returned, table, xall, w_gate_one, w_up_one, w_down_one)
        r = exchange_sums((s0, s1, s2, s3))
        grads_one = weight_grads(*rows_one)
        dx_tokens = (dy_mid.astype(F32) + ((r[0] + r[1]) + (r[2] + r[3]))).astype(BF16)
        return (dx_tokens, *grads_one, *grads_two)

    return jax.shard_map(local_step, mesh=mesh, in_specs=(tok_spec,) * 9 + (weight_spec,) * 6, out_specs=(tok_spec,) + (grad_spec,) * 6, check_vma=False)
```

time: 153 us -> 113 us (0.74)
  local copies, waits for them, and re-layouts: 19.7 us -> 0.01 us
  Pallas kernels: 122 us -> 104 us
  other arithmetic: 2.89 us -> 0.78 us
    unnamed x34 -> x6, local copies, waits for them, and re-layouts: 18.6 us -> 0.01 us
    pallas_call x1, Pallas kernels: 51.4 us -> 42.5 us  [layer_two(): pl.pallas_call(layer_two_kernel, name='layer_two', out_shape=ROW_OUTS + [...]
    pallas_call x1, Pallas kernels: 32.8 us -> 26.7 us  [layer_one(): pl.pallas_call(layer_one_kernel, name='layer_one', out_shape=ROW_OUTS + [...]
    pallas_call x2, Pallas kernels: 37.4 us -> 35.1 us  [weight_grads(): pl.pallas_call(weight_grad_kernel, name='weight_grads', in_specs=[HBM_SPE...]
  transfers between devices with their start and end apart: 6 -> 6, of which waited for: 0 -> 0; matrix products, arithmetic and copies ran while one was open for 0% -> 0% of each run, Pallas kernels for 25% -> 31%
where the time goes in v2:
time: 113 us
  Pallas kernels  104 us (92%)
  starting transfers between devices  7.02 us (6%)
    pallas_call x1, Pallas kernels, layer_two(): pl.pallas_call(layer_two_kernel, name='layer_two', out_shape=ROW_OUTS + [...  42.5 us
    pallas_call x2, Pallas kernels, weight_grads(): pl.pallas_call(weight_grad_kernel, name='weight_grads', in_specs=[HBM_SPE...  35.1 us
    pallas_call x1, Pallas kernels, layer_one(): pl.pallas_call(layer_one_kernel, name='layer_one', out_shape=ROW_OUTS + [...  26.7 us
    ppermute x6, starting transfers between devices, exchange_sums(): lax.ppermute(sums[k], 'expert', swap(mask))  7.02 us
  transfers between devices with their start and end apart: 6, of which 0 were waited for; matrix products, arithmetic and copies ran while one was open for 0% of the time, Pallas kernels for 31%

profile of v2, /device:TPU:0, one launch (start us, length us, event | category | flops | bytes accessed | tf_op | source)
XLA Modules:
  0.0 112.9 jit_solution(16466419109506574011)
XLA Ops:
  0.6 42.5 %layer_two.1 = (bf16[5,192,1536]{2,1,0:T(8,128)(2,1)}, bf16[5,192,1536]{2,1,0:T(8,128)(2,1)}, bf16[5,192,512]{2,1,0:T(8,128)(2,1)}, bf16[5,192,512]{2,1,0:T(8,12...) custom-call(s32[8,64]{1,0:T(8,128)} %bitcast.6, ...), custom_call_target="tpu_custom_call" | custom-call | flops 16000000000 | bytes 37748736 | tf_op jit(solution)/shard_map/layer_two/pallas_call | solution.py:400
  43.1 1.5 %collective-permute-start = (f32[64,1536]{1,0:T(8,128)}, f32[64,1536]{1,0:T(8,128)S(1)}, u32[]{:S(2)}, u32[]{:S(2)}) collective-permute-start(f32[64,1536]{1,0:T(8,128)} %get-tuple-element.35), channel_id=1, source_target_pairs={{0,2},{1,3},{2,0},{3,1},{4,6},{5,7},{6,4},{7,5}} | collective-permute-start | bytes 1179656 | tf_op jit(solution)/shard_map/ppermute | solution.py:482
  44.6 0.6 collective-permute-start.1
  45.2 1.5 %collective-permute-start.2 = (f32[64,1536]{1,0:T(8,128)}, f32[64,1536]{1,0:T(8,128)S(1)}, u32[]{:S(2)}, u32[]{:S(2)}) collective-permute-start(f32[64,1536]{1,0:T(8,128)} %get-tuple-element.37), channel_id=1, source_target_pairs={{0,6},{1,7},{2,4},{3,5},{4,2},{5,3},{6,0},{7,1}} | collective-permute-start | bytes 1179656 | tf_op jit(solution)/shard_map/ppermute | solution.py:482
  46.6 0.0 copy-start
  46.6 0.0 copy-start.1
  46.6 0.0 copy-start.2
  46.6 17.7 %weight_grads.3 = (f32[5,1536,512]{2,1,0:T(8,128)}, f32[5,1536,512]{2,1,0:T(8,128)}, f32[5,512,1536]{2,1,0:T(8,128)}) custom-call(bf16[5,192,1536]{2,1,0:T(8,128)(2,1)} %get-tuple-element.53.u_h, bf16[5,192,1536]{2,1,0:T(8,128)(2,1)} %get-tuple-element.54.z_h, bf16[5,192,512]{2,1,0:T(8,128)(2,1)} %get-tuple-element.55.hid_h, ...), custom_call_target="tpu_custom_call" | custom-call | flops 17999998976 | bytes 58720256 | tf_op jit(solution)/shard_map/weight_grads/pallas_call | solution.py:470
  64.3 0.0 collective-permute-done.r_x
  64.3 0.0 collective-permute-done.1.r_y
  64.4 0.0 collective-permute-done.2.r_d
  64.4 0.0 copy-done
  64.4 0.0 copy-done.1
  64.4 0.0 copy-done.2
  64.4 26.7 %layer_one.1 = (bf16[5,192,1536]{2,1,0:T(8,128)(2,1)}, bf16[5,192,1536]{2,1,0:T(8,128)(2,1)}, bf16[5,192,512]{2,1,0:T(8,128)(2,1)}, bf16[5,192,512]{2,1,0:T(8,12...) custom-call(bf16[64,1536]{1,0:T(8,128)(2,1)S(1)} %copy-done, ...), custom_call_target="tpu_custom_call" | custom-call | flops 16000000000 | bytes 37748736 | tf_op jit(solution)/shard_map/layer_one/pallas_call | solution.py:413
  91.1 0.7 collective-permute-start.3
  91.9 1.3 %collective-permute-start.4 = (f32[64,1536]{1,0:T(8,128)S(1)}, f32[64,1536]{1,0:T(8,128)S(1)}, u32[]{:S(2)}, u32[]{:S(2)}) collective-permute-start(f32[64,1536]{1,0:T(8,128)S(1)} %get-tuple-element.43), channel_id=1, source_target_pairs={{0,4},{1,5},{2,6},{3,7},{4,0},{5,1},{6,2},{7,3}} | collective-permute-start | bytes 1179656 | tf_op jit(solution)/shard_map/ppermute | solution.py:482
  93.2 1.5 %collective-permute-start.5 = (f32[64,1536]{1,0:T(8,128)S(1)}, f32[64,1536]{1,0:T(8,128)S(1)}, u32[]{:S(2)}, u32[]{:S(2)}) collective-permute-start(f32[64,1536]{1,0:T(8,128)S(1)} %get-tuple-element.44), channel_id=1, source_target_pairs={{0,6},{1,7},{2,4},{3,5},{4,2},{5,3},{6,0},{7,1}} | collective-permute-start | bytes 1179656 | tf_op jit(solution)/shard_map/ppermute | solution.py:482
  94.6 17.4 %weight_grads.2 = (f32[5,1536,512]{2,1,0:T(8,128)}, f32[5,1536,512]{2,1,0:T(8,128)}, f32[5,512,1536]{2,1,0:T(8,128)}) custom-call(bf16[5,192,1536]{2,1,0:T(8,128)(2,1)} %get-tuple-element.45.u_h, bf16[5,192,1536]{2,1,0:T(8,128)(2,1)} %get-tuple-element.46.z_h, bf16[5,192,512]{2,1,0:T(8,128)(2,1)} %get-tuple-element.47.hid_h, ...), custom_call_target="tpu_custom_call" | custom-call | flops 17999998976 | bytes 58720256 | tf_op jit(solution)/shard_map/weight_grads/pallas_call | solution.py:470
  112.1 0.0 collective-permute-done.3
  112.1 0.0 collective-permute-done.4
  112.1 0.0 collective-permute-done.5
  112.1 0.8 add_convert_fusion
Async XLA Ops:
  43.1 21.2 %collective-permute-start = (f32[64,1536]{1,0:T(8,128)}, f32[64,1536]{1,0:T(8,128)S(1)}, u32[]{:S(2)}, u32[]{:S(2)}) collective-permute-start(f32[64,1536]{1,0:T(8,128)} %get-tuple-element.35), channel_id=1, source_target_pairs={{0,2},{1,3},{2,0},{3,1},{4,6},{5,7},{6,4},{7,5}} | collective-permute-start | bytes 1179656 | tf_op jit(solution)/shard_map/ppermute | solution.py:482
  44.6 19.7 %collective-permute-start.1 = (f32[64,1536]{1,0:T(8,128)}, f32[64,1536]{1,0:T(8,128)S(1)}, u32[]{:S(2)}, u32[]{:S(2)}) collective-permute-start(f32[64,1536]{1,0:T(8,128)} %get-tuple-element.36), channel_id=1, source_target_pairs={{0,4},{1,5},{2,6},{3,7},{4,0},{5,1},{6,2},{7,3}} | collective-permute-start | bytes 1179656 | tf_op jit(solution)/shard_map/ppermute | solution.py:482
  45.2 19.2 %collective-permute-start.2 = (f32[64,1536]{1,0:T(8,128)}, f32[64,1536]{1,0:T(8,128)S(1)}, u32[]{:S(2)}, u32[]{:S(2)}) collective-permute-start(f32[64,1536]{1,0:T(8,128)} %get-tuple-element.37), channel_id=1, source_target_pairs={{0,6},{1,7},{2,4},{3,5},{4,2},{5,3},{6,0},{7,1}} | collective-permute-start | bytes 1179656 | tf_op jit(solution)/shard_map/ppermute | solution.py:482
  46.6 17.7 %copy-start = (bf16[64,1536]{1,0:T(8,128)(2,1)S(1)}, bf16[64,1536]{1,0:T(8,128)(2,1)}, u32[]{:S(2)}) copy-start(bf16[64,1536]{1,0:T(8,128)(2,1)} %dy_h.1) | copy-start | bytes 589828
  46.6 17.8 %copy-start.1 = (f32[64,1536]{1,0:T(8,128)S(1)}, f32[64,1536]{1,0:T(8,128)}, u32[]{:S(2)}) copy-start(f32[64,1536]{1,0:T(8,128)} %get-tuple-element.34.r_me) | copy-start | bytes 1179652
  46.6 17.8 %copy-start.2 = (f32[32,512]{1,0:T(8,128)S(1)}, f32[32,512]{1,0:T(8,128)}, u32[]{:S(2)}) copy-start(f32[32,512]{1,0:T(8,128)} %get-tuple-element.38.table) | copy-start | bytes 196612
  91.1 21.0 %collective-permute-start.3 = (f32[64,1536]{1,0:T(8,128)S(1)}, f32[64,1536]{1,0:T(8,128)S(1)}, u32[]{:S(2)}, u32[]{:S(2)}) collective-permute-start(f32[64,1536]{1,0:T(8,128)S(1)} %get-tuple-element.42), channel_id=1, source_target_pairs={{0,2},{1,3},{2,0},{3,1},{4,6},{5,7},{6,4},{7,5}} | collective-permute-start | bytes 1179656 | tf_op jit(solution)/shard_map/ppermute | solution.py:482
  91.9 20.2 %collective-permute-start.4 = (f32[64,1536]{1,0:T(8,128)S(1)}, f32[64,1536]{1,0:T(8,128)S(1)}, u32[]{:S(2)}, u32[]{:S(2)}) collective-permute-start(f32[64,1536]{1,0:T(8,128)S(1)} %get-tuple-element.43), channel_id=1, source_target_pairs={{0,4},{1,5},{2,6},{3,7},{4,0},{5,1},{6,2},{7,3}} | collective-permute-start | bytes 1179656 | tf_op jit(solution)/shard_map/ppermute | solution.py:482
  93.2 19.0 %collective-permute-start.5 = (f32[64,1536]{1,0:T(8,128)S(1)}, f32[64,1536]{1,0:T(8,128)S(1)}, u32[]{:S(2)}, u32[]{:S(2)}) collective-permute-start(f32[64,1536]{1,0:T(8,128)S(1)} %get-tuple-element.44), channel_id=1, source_target_pairs={{0,6},{1,7},{2,4},{3,5},{4,2},{5,3},{6,0},{7,1}} | collective-permute-start | bytes 1179656 | tf_op jit(solution)/shard_map/ppermute | solution.py:482

commit v3 on v2

--- a/solution.py
+++ b/solution.py
@@ -17,6 +17,8 @@
 HALF_ROWS = 4 * CAP
 ROWS = 8 * CAP
 STEP = 512
+SLOTS = 512
+CHUNKS = ((0, 768), (768, 512), (1280, 256))
 
 
 def place():
@@ -38,11 +40,13 @@
     return ids, core, x, y
 
 
-def barrier(ids):
-    sem = pltpu.get_barrier_semaphore()
+def greet(ids):
     for peer in ("partner", "x", "y"):
-        pl.semaphore_signal(sem, inc=1, device_id={"expert": ids[peer]}, device_id_type=MESH)
-    pl.semaphore_wait(sem, 3)
+        pl.semaphore_signal(pltpu.get_barrier_semaphore(), inc=1, device_id={"expert": ids[peer]}, device_id_type=MESH)
+
+
+def await_peers():
+    pl.semaphore_wait(pltpu.get_barrier_semaphore(), 3)
 
 
 def block(ref, ident):
@@ -62,10 +66,13 @@
         size = TOK // self.pieces
         return self.ref.at[pl.ds(pl.multiple_of(ident * TOK + i * size, size), size)]
 
+    def arrival(self, k, i):
+        return self.recv.at[3 * i + k - 1] if 1 <= k <= 3 else self.recv.at[3 * max(self.pieces, 1)]
+
     def copy(self, k, i, what=None, where=None):
         what, where = what or self.ROUTES[k][0], where or self.ROUTES[k][1]
         part = self.part(self.ids[what], i)
-        return pltpu.make_async_remote_copy(src_ref=part, dst_ref=part, send_sem=self.send.at[i, k], recv_sem=self.recv.at[i, k], device_id={"expert": self.ids[where]}, device_id_type=MESH)
+        return pltpu.make_async_remote_copy(src_ref=part, dst_ref=part, send_sem=self.send.at[0], recv_sem=self.arrival(k, i), device_id={"expert": self.ids[where]}, device_id_type=MESH)
 
     def arrived(self, k, i):
         self.copy(k, i, self.ARRIVE[k], "partner").wait_recv()
@@ -88,15 +95,15 @@
         self.arrived(3, i)
         self.copy(6, i).start()
 
+    def blocks(self, count):
+        part = self.ref.at[pl.ds(0, count * (TOK if self.pieces else 1))]
+        return pltpu.make_async_remote_copy(src_ref=part, dst_ref=part, send_sem=self.send.at[0], recv_sem=self.recv.at[3 * max(self.pieces, 1)], device_id={"expert": self.ids["partner"]}, device_id_type=MESH)
+
     def finish(self):
-        for i in self.every():
-            for k in (0, 4, 5, 6):
-                self.arrived(k, i)
+        self.blocks(4).wait_recv()
 
     def drain(self):
-        for i in self.every():
-            for k in range(7):
-                self.copy(k, i).wait_send()
+        self.blocks(7).wait_send()
 
 
 PARTNER, PRIM, SEC = 0, 1, 2
@@ -119,6 +126,7 @@
 
 def build_onehot(table, base, me, onehot, gate_col):
     for h in range(2):
+        onehot[h, LOCAL * HALF_ROWS : SLOTS, :] = jnp.zeros((SLOTS - LOCAL * HALF_ROWS, 256), BF16)
         cols = slice(h * 256, (h + 1) * 256)
         keys = [table[base + j : base + j + 1, cols] for j in range(8)]
         gates = [table[base + 8 + j : base + 9 + j, cols] for j in range(8)]
@@ -134,11 +142,26 @@
             gate_col[h, e * HALF_ROWS : (e + 1) * HALF_ROWS, :] = jnp.broadcast_to(jnp.sum(gate, axis=1, keepdims=True), (HALF_ROWS, 128))
 
 
+def build_scatter(onehot, scatter):
+    for h in range(2):
+        scatter[h] = jnp.transpose(onehot[h])
+
+
+def turn_tall(src, dst, e):
+    for n in range(D // 128):
+        dst[e, :, n * 128 : (n + 1) * 128] = jnp.transpose(src[e, n * 128 : (n + 1) * 128, :])
+
+
+def turn_wide(src, dst, e):
+    for n in range(D // 128):
+        dst[e, n * 128 : (n + 1) * 128, :] = jnp.transpose(src[e, :, n * 128 : (n + 1) * 128])
+
+
 def take_rows(onehot, tokens, rows, gate_col=None):
     for h in range(2):
         for n in range(D // STEP):
             cols = slice(n * STEP, (n + 1) * STEP)
-            out = jnp.dot(onehot[h], tokens[h * 256 : (h + 1) * 256, cols], preferred_element_type=F32)
+            out = jnp.dot(onehot[h, 0 : LOCAL * HALF_ROWS], tokens[h * 256 : (h + 1) * 256, cols], preferred_element_type=F32)
             if gate_col is not None:
                 out = out * gate_col[h, :, 0:1]
             out = out.astype(BF16)
@@ -160,7 +183,7 @@
 
 
 def hidden_grads(e, z, w2, a, b):
-    dh = lax.dot_general(z[e], w2[e], TRANS_B, preferred_element_type=F32)
+    dh = jnp.dot(z[e], w2[e], preferred_element_type=F32)
     act = a[e].astype(F32)
     up = b[e].astype(F32)
     sig = jax.nn.sigmoid(act)
@@ -168,51 +191,55 @@
     b[e] = (dh * (act * sig)).astype(BF16)
 
 
-def row_grads(e, cols, w1, w3, a, b, dxr):
-    dx = lax.dot_general(a[e], w1[e, cols, :], TRANS_B, preferred_element_type=F32) + lax.dot_general(b[e], w3[e, cols, :], TRANS_B, preferred_element_type=F32)
+def row_grads(e, cols, turned, w1, w3, a, b, dxr):
+    if turned:
+        dx = jnp.dot(a[e], w1[e, :, cols], preferred_element_type=F32) + jnp.dot(b[e], w3[e, :, cols], preferred_element_type=F32)
+    else:
+        dx = lax.dot_general(a[e], w1[e, cols, :], TRANS_B, preferred_element_type=F32) + lax.dot_general(b[e], w3[e, cols, :], TRANS_B, preferred_element_type=F32)
     dx = dx.astype(BF16)
     for h in range(2):
-        dxr[h, e * HALF_ROWS : (e + 1) * HALF_ROWS, cols] = dx[h * HALF_ROWS : (h + 1) * HALF_ROWS]
-
-
-def return_sums(ids, core, x, y, onehot, w1, w3, a, b, dxr, sums, inbox, send, recv, ssem, outs, between):
+        dxr[e * HALF_ROWS : (e + 1) * HALF_ROWS, h * (D // 2) : h * (D // 2) + dx.shape[1]] = dx[h * HALF_ROWS : (h + 1) * HALF_ROWS]
+
+
+def return_sums(ids, core, x, y, scatter, turned, w1, w3, a, b, dxr, sums, inbox, send, recv, ssem, outs, between):
     def exchange(n, yy, xx):
         theirs = 4 * yy + 2 * xx + (1 - core)
-        cols = pl.ds(n * STEP, STEP)
+        cols = pl.ds(*CHUNKS[n])
         src = sums.at[pl.ds(pl.multiple_of(theirs * TOK, TOK), TOK), cols]
-        return pltpu.make_async_remote_copy(src_ref=src, dst_ref=inbox.at[2 * yy + xx, :, cols], send_sem=send.at[n, 2 * yy + xx], recv_sem=recv.at[n, 2 * yy + xx], device_id={"expert": ids["partner"]}, device_id_type=MESH)
+        return pltpu.make_async_remote_copy(src_ref=src, dst_ref=inbox.at[2 * yy + xx, :, cols], send_sem=send.at[0], recv_sem=recv.at[n], device_id={"expert": ids["partner"]}, device_id_type=MESH)
+
+    def whole(ref, sem):
+        return pltpu.make_async_remote_copy(src_ref=ref, dst_ref=ref, send_sem=send.at[0], recv_sem=sem, device_id={"expert": ids["partner"]}, device_id_type=MESH)
 
     def store(n, name, xx, yy, out, k):
-        cols = pl.ds(n * STEP, STEP)
-        return pltpu.make_async_copy(inbox.at[2 * yy + xx, :, cols], out.at[:, cols], ssem.at[n, k])
+        cols = pl.ds(*CHUNKS[n])
+        return pltpu.make_async_copy(inbox.at[2 * yy + xx, :, cols], out.at[:, cols], ssem.at[k])
 
     blocks = (("me", x, y, outs[0], 0), ("x", 1 - x, y, outs[1], 1), ("y", x, 1 - y, outs[2], 2), ("diag", 1 - x, 1 - y, outs[3], 3))
 
     def collect(n):
-        for k in range(4):
-            exchange(n, k // 2, k % 2).wait_recv()
-        cols = slice(n * STEP, (n + 1) * STEP)
+        cols = slice(CHUNKS[n][0], sum(CHUNKS[n]))
+        whole(inbox.at[:, :, cols], recv.at[n]).wait_recv()
         for name, xx, yy, out, k in blocks:
             inbox[2 * yy + xx, :, cols] = inbox[2 * yy + xx, :, cols] + sums[pl.ds(pl.multiple_of(ids[name] * TOK, TOK), TOK), cols]
             store(n, name, xx, yy, out, k).start()
 
-    for n in range(D // STEP):
-        cols = slice(n * STEP, (n + 1) * STEP)
+    for n in range(len(CHUNKS)):
+        cols = slice(CHUNKS[n][0], sum(CHUNKS[n]))
         for e in range(LOCAL):
-            row_grads(e, cols, w1, w3, a, b, dxr)
+            row_grads(e, cols, turned, w1, w3, a, b, dxr)
         for h in range(2):
-            sums[h * 256 : (h + 1) * 256, cols] = lax.dot_general(onehot[h], dxr[h, :, cols], TRANS_A, preferred_element_type=F32)
+            sums[h * 256 : (h + 1) * 256, cols] = jnp.dot(scatter[h, :, 0 : LOCAL * HALF_ROWS], dxr[0 : LOCAL * HALF_ROWS, h * (D // 2) : h * (D // 2) + CHUNKS[n][1]], preferred_element_type=F32)
         for k in range(4):
             exchange(n, k // 2, k % 2).start()
-        if n > 0:
-            collect(n - 1)
+        if n == 2:
+            collect(0)
         between(n)
-    collect(D // STEP - 1)
-    for n in range(D // STEP):
-        for k in range(4):
-            exchange(n, k // 2, k % 2).wait_send()
-        for entry in blocks:
-            store(n, *entry).wait()
+    collect(1)
+    collect(2)
+    whole(inbox, recv.at[0]).wait_send()
+    for name, xx, yy, out, k in blocks:
+        pltpu.make_async_copy(inbox.at[2 * yy + xx], out, ssem.at[k]).wait()
 
 
 class Weights:
@@ -237,9 +264,10 @@
     (y_h, dy_h, x_h, w1_h, w3_h, w2_h,
      u_o, z_o, hid_o, da_o, db_o, xall_o, table_o, s_me, s_x, s_y, s_d) = refs[:17]
     routing, refs = refs[17:23], refs[23:]
-    (tab, yall, dall, xall, w1, w3, w2, onehot, gate_col, u, z, a, b, hid, dxr, sums, inbox,
+    (tab, yall, dall, xall, w1, w3, w2, onehot, scatter, gate_col, w2t, u, z, a, b, hid, sums, inbox, w3t, table,
      lsem, wsem, osem, tsend, trecv, gsend, grecv, xsend, xrecv, ssem) = refs
     ids, core, x, y = place()
+    greet(ids)
     small = [pltpu.make_async_copy(src, dst, lsem.at[3 + i]) for i, (src, dst) in enumerate(zip(routing_h, routing))]
     local = [pltpu.make_async_copy(src, block(dst, ids["me"]), lsem.at[i]) for i, (src, dst) in enumerate(((y_h, yall), (dy_h, dall), (x_h, xall)))]
     for c in small + local:
@@ -247,58 +275,84 @@
     for c in small:
         c.wait()
     fill_table(routing, ids["me"], tab.at[ids["me"]])
-    for c in local:
-        c.wait()
+    local[0].wait()
     weights = Weights((w1_h, w3_h, w2_h), (w1, w3, w2), wsem)
-    weights.start((0, 1, 2), range(LOCAL))
-    barrier(ids)
     gt = Gather(ids, tab, tsend, trecv, 0)
     gy, gd, gx = [Gather(ids, ref, gsend.at[i], grecv.at[i], 2) for i, ref in enumerate((yall, dall, xall))]
-    for k in (PRIM, SEC, PARTNER):
-        gt.start(k)
-    for k in (PRIM, SEC, PARTNER):
-        gy.start(k)
-    for k in (PRIM, PARTNER):
-        gd.start(k)
+    await_peers()
+    gt.start(PRIM)
+    gt.start(SEC)
+    gy.start(PRIM)
+    gt.start(PARTNER)
+    for c in local[1:]:
+        c.wait()
+    weights.start((2,), range(LOCAL))
+    weights.start((0, 1), range(LOCAL))
+
+    def turn(first, last):
+        for i in range(first, last):
+            e = i % LOCAL
+            if i < 2 * LOCAL:
+                weights.wait(((2,), (0,))[i // LOCAL], e)
+            (turn_wide, turn_tall, turn_tall)[i // LOCAL]((w2, w1, w3)[i // LOCAL], (w2t, w2, w3t)[i // LOCAL], e)
+
+    turn(0, 1)
+    gy.start(PARTNER)
+    turn(1, 2)
+    gy.start(SEC)
+    turn(2, 3)
     gt.relay_prim(0)
     gy.relay_prim(0)
+    turn(3, 5)
+    gy.relay_prim(1)
+    turn(5, 8)
+    gd.start(PRIM)
     gt.relay_rest(0)
+    turn(8, 9)
     gt.finish()
-    gy.relay_prim(1)
+    join_table(tab, table)
+    save_table = pltpu.make_async_copy(table, table_o, osem.at[6])
+    save_table.start()
+    build_onehot(table, 0, ids["me"], onehot, gate_col)
     gd.start(SEC)
-    join_table(tab, table_o)
-    build_onehot(table_o, 0, ids["me"], onehot, gate_col)
+    gd.start(PARTNER)
     gy.relay_rest(0)
+    build_scatter(onehot, scatter)
+    turn(9, 10)
     gy.relay_rest(1)
+    for e in range(LOCAL):
+        weights.wait((1,), e)
+    turn(10, 11)
     gy.finish()
+    gd.relay_prim(0)
     take_rows(onehot, yall, u)
     store_u = pltpu.make_async_copy(u, u_o, osem.at[0])
     store_u.start()
 
     def forward(first, last):
-        for e in range(first, last):
-            weights.wait((0, 1), e)
-            forward_expert(e, u, w1, w3, a, b, hid)
-
-    forward(0, 1)
-    gd.relay_prim(0)
+        lax.fori_loop(first, last, lambda e, carry: (forward_expert(e, u, w1, w3, a, b, hid), carry)[1], 0)
+
     gd.relay_prim(1)
-    for k in (PRIM, SEC, PARTNER):
-        gx.start(k)
-    forward(1, LOCAL)
+    forward(0, 2)
+    gx.start(PRIM)
+    forward(2, 4)
+    gx.start(SEC)
+    forward(4, LOCAL)
     gd.relay_rest(0)
+    turn(11, 13)
     gd.relay_rest(1)
+    turn(13, 3 * LOCAL)
+    gx.relay_prim(0)
     gd.finish()
+    gx.start(PARTNER)
     take_rows(onehot, dall, z, gate_col)
-    gx.relay_prim(0)
     store_z = pltpu.make_async_copy(z, z_o, osem.at[1])
     store_h = pltpu.make_async_copy(hid, hid_o, osem.at[2])
     store_z.start()
     store_h.start()
+    gx.relay_prim(1)
     for e in range(LOCAL):
-        weights.wait((2,), e)
-        hidden_grads(e, z, w2, a, b)
-    gx.relay_prim(1)
+        hidden_grads(e, z, w2t, a, b)
     store_a = pltpu.make_async_copy(a, da_o, osem.at[3])
     store_b = pltpu.make_async_copy(b, db_o, osem.at[4])
     store_a.start()
@@ -306,48 +360,54 @@
     store_x = pltpu.make_async_copy(xall, xall_o, osem.at[5])
 
     def between(n):
-        if n == 0:
+        if n == 1:
             gx.relay_rest(0)
             gx.relay_rest(1)
-        if n == 1:
+        if n == 2:
             gx.finish()
             store_x.start()
 
-    return_sums(ids, core, x, y, onehot, w1, w3, a, b, dxr, sums, inbox, xsend, xrecv, ssem, (s_me, s_x, s_y, s_d), between)
-    for g in (gt, gy, gd, gx):
+    gy.drain()
+    return_sums(ids, core, x, y, scatter, True, w2, w3t, a, b, yall, sums, inbox, xsend, xrecv, ssem, (s_me, s_x, s_y, s_d), between)
+    for g in (gt, gd, gx):
         g.drain()
-    for c in (store_u, store_z, store_h, store_a, store_b, store_x):
+    for c in (store_u, store_z, store_h, store_a, store_b, store_x, save_table):
         c.wait()
 
 
 def layer_one_kernel(dy_h, r_me, r_x, r_y, r_d, table, xall_h, w1_h, w3_h, w2_h,
                      u_o, z_o, hid_o, da_o, db_o, dy1_o, s_me, s_x, s_y, s_d,
-                     dall, xall, w1, w3, w2, onehot, gate_col, u, z, a, b, hid, dxr, sums, inbox,
+                     dall, xall, w1, w3, w2, onehot, scatter, gate_col, w2t, u, z, a, b, hid, sums, inbox,
                      lsem, wsem, osem, gsend, grecv, xsend, xrecv, ssem):
     ids, core, x, y = place()
+    greet(ids)
     load_x = pltpu.make_async_copy(xall_h, xall, lsem.at[0])
     load_x.start()
     weights = Weights((w1_h, w3_h, w2_h), (w1, w3, w2), wsem)
     dy1 = (dy_h[...].astype(F32) + ((r_me[...] + r_x[...]) + (r_y[...] + r_d[...]))).astype(BF16)
     dall[pl.ds(pl.multiple_of(ids["me"] * TOK, TOK), TOK), :] = dy1
     dy1_o[...] = dy1
-    barrier(ids)
+    await_peers()
     gd = Gather(ids, dall, gsend, grecv, 2)
-    for k in (PRIM, SEC, PARTNER):
-        gd.start(k)
+    gd.start(PRIM)
     load_x.wait()
     weights.start((0, 1), (0, 1))
     build_onehot(table, 16, ids["me"], onehot, gate_col)
     weights.start((0, 1), (2, 3, 4))
     take_rows(onehot, xall, u)
     weights.start((2,), range(LOCAL))
+    gd.start(SEC)
+    gd.start(PARTNER)
+    build_scatter(onehot, scatter)
     store_u = pltpu.make_async_copy(u, u_o, osem.at[0])
     store_u.start()
 
     def forward(first, last):
-        for e in range(first, last):
+        def step(e, carry):
             weights.wait((0, 1), e)
             forward_expert(e, u, w1, w3, a, b, hid)
+            return carry
+        lax.fori_loop(first, last, step, 0)
 
     forward(0, 1)
     gd.relay_prim(0)
@@ -355,6 +415,9 @@
     gd.relay_prim(1)
     forward(2, LOCAL)
     gd.relay_rest(0)
+    for e in range(LOCAL):
+        weights.wait((2,), e)
+        turn_wide(w2, w2t, e)
     gd.relay_rest(1)
     gd.finish()
     take_rows(onehot, dall, z, gate_col)
@@ -363,29 +426,28 @@
     store_z.start()
     store_h.start()
     for e in range(LOCAL):
-        weights.wait((2,), e)
-        hidden_grads(e, z, w2, a, b)
+        hidden_grads(e, z, w2t, a, b)
     store_a = pltpu.make_async_copy(a, da_o, osem.at[3])
     store_b = pltpu.make_async_copy(b, db_o, osem.at[4])
     store_a.start()
     store_b.start()
-    return_sums(ids, core, x, y, onehot, w1, w3, a, b, dxr, sums, inbox, xsend, xrecv, ssem, (s_me, s_x, s_y, s_d), lambda n: None)
+    return_sums(ids, core, x, y, scatter, False, w1, w3, a, b, xall, sums, inbox, xsend, xrecv, ssem, (s_me, s_x, s_y, s_d), lambda n: None)
     gd.drain()
     for c in (store_u, store_z, store_h, store_a, store_b):
         c.wait()
 
 
-HBM_SPEC = pl.BlockSpec(memory_space=pl.ANY)
+HBM_SPEC = pl.BlockSpec(memory_space=pltpu.HBM)
 VMEM_SPEC = pl.BlockSpec(memory_space=pltpu.VMEM)
 
 
 def compute_scratch():
     return [
         pltpu.VMEM((LOCAL, D, F), BF16), pltpu.VMEM((LOCAL, D, F), BF16), pltpu.VMEM((LOCAL, F, D), BF16),
-        pltpu.VMEM((2, LOCAL * HALF_ROWS, 256), BF16), pltpu.VMEM((2, LOCAL * HALF_ROWS, 128), F32),
+        pltpu.VMEM((2, SLOTS, 256), BF16), pltpu.VMEM((2, 256, SLOTS), BF16), pltpu.VMEM((2, LOCAL * HALF_ROWS, 128), F32), pltpu.VMEM((LOCAL, D, F), BF16),
         pltpu.VMEM((LOCAL, ROWS, D), BF16), pltpu.VMEM((LOCAL, ROWS, D), BF16),
         pltpu.VMEM((LOCAL, ROWS, F), BF16), pltpu.VMEM((LOCAL, ROWS, F), BF16), pltpu.VMEM((LOCAL, ROWS, F), BF16),
-        pltpu.VMEM((2, LOCAL * HALF_ROWS, D), BF16), pltpu.VMEM((8 * TOK, D), F32), pltpu.VMEM((4, TOK, D), F32),
+        pltpu.VMEM((8 * TOK, D), F32), pltpu.VMEM((4, TOK, D), F32),
     ]
 
 
@@ -400,10 +462,10 @@
     return pl.pallas_call(
         layer_two_kernel, name="layer_two",
         out_shape=ROW_OUTS + [jax.ShapeDtypeStruct((8 * TOK, D), BF16), jax.ShapeDtypeStruct((32, 8 * TOK), F32)] + SUM_OUTS,
-        in_specs=[HBM_SPEC] * 12, out_specs=[HBM_SPEC] * 6 + [VMEM_SPEC] + [HBM_SPEC] * 4,
-        scratch_shapes=table_in * 2 + [pltpu.VMEM((8, 32, 128), F32), all_tok, all_tok, all_tok] + compute_scratch()
-        + [DMA((9,)), DMA((3, LOCAL)), DMA((6,)), DMA((1, 7)), DMA((1, 7)), DMA((3, 2, 7)), DMA((3, 2, 7)), DMA((3, 4)), DMA((3, 4)), DMA((3, 4))],
-        compiler_params=pltpu.CompilerParams(collective_id=0, has_side_effects=True, vmem_limit_bytes=56 * 2**20),
+        in_specs=[HBM_SPEC] * 12, out_specs=[HBM_SPEC] * 11,
+        scratch_shapes=table_in * 2 + [pltpu.VMEM((8, 32, 128), F32), all_tok, all_tok, all_tok] + compute_scratch() + [pltpu.VMEM((LOCAL, F, D), BF16), pltpu.VMEM((32, 8 * TOK), F32)]
+        + [DMA((9,)), DMA((3, LOCAL)), DMA((7,)), DMA((1,)), DMA((4,)), DMA((3, 1)), DMA((3, 7)), DMA((1,)), DMA((len(CHUNKS),)), DMA((4,))],
+        compiler_params=pltpu.CompilerParams(collective_id=0, has_side_effects=True, vmem_limit_bytes=63 * 2**20),
         cost_estimate=pl.CostEstimate(flops=16 * 10**9, bytes_accessed=36 * 2**20, transcendentals=0),
     )(*routing, y_mid, dy_out, x_tokens, w1, w3, w2)
 
@@ -415,7 +477,7 @@
         out_shape=ROW_OUTS + [jax.ShapeDtypeStruct((TOK, D), BF16)] + SUM_OUTS,
         in_specs=[VMEM_SPEC] * 6 + [HBM_SPEC] * 4, out_specs=[HBM_SPEC] * 5 + [VMEM_SPEC] + [HBM_SPEC] * 4,
         scratch_shapes=[all_tok, all_tok] + compute_scratch()
-        + [DMA((1,)), DMA((3, LOCAL)), DMA((5,)), DMA((2, 7)), DMA((2, 7)), DMA((3, 4)), DMA((3, 4)), DMA((3, 4))],
+        + [DMA((1,)), DMA((3, LOCAL)), DMA((5,)), DMA((1,)), DMA((7,)), DMA((1,)), DMA((len(CHUNKS),)), DMA((4,))],
         compiler_params=pltpu.CompilerParams(collective_id=1, has_side_effects=True, vmem_limit_bytes=50 * 2**20),
         cost_estimate=pl.CostEstimate(flops=16 * 10**9, bytes_accessed=36 * 2**20, transcendentals=0),
     )(dy_out, *returned, table, xall, w1, w3, w2)

time: 113 us -> 102 us (0.903)
  Pallas kernels: 104 us -> 93.8 us
    pallas_call x1, Pallas kernels: 42.5 us -> 33.9 us  [layer_two(): pl.pallas_call(layer_two_kernel, name='layer_two', out_shape=ROW_OUTS + [...]
    pallas_call x1, Pallas kernels: 26.7 us -> 24.8 us  [layer_one(): pl.pallas_call(layer_one_kernel, name='layer_one', out_shape=ROW_OUTS + [...]
  transfers between devices with their start and end apart: 6 -> 6, of which waited for: 0 -> 0; matrix products, arithmetic and copies ran while one was open for 0% -> 0% of each run, Pallas kernels for 31% -> 34%
where the time goes in v3:
time: 102 us
  Pallas kernels  93.8 us (92%)
  starting transfers between devices  7.02 us (7%)
    pallas_call x2, Pallas kernels, weight_grads(): pl.pallas_call(weight_grad_kernel, name='weight_grads', in_specs=[HBM_SPE...  35.1 us
    pallas_call x1, Pallas kernels, layer_two(): pl.pallas_call(layer_two_kernel, name='layer_two', out_shape=ROW_OUTS + [...  33.9 us
    pallas_call x1, Pallas kernels, layer_one(): pl.pallas_call(layer_one_kernel, name='layer_one', out_shape=ROW_OUTS + [...  24.8 us
    ppermute x6, starting transfers between devices, exchange_sums(): lax.ppermute(sums[k], 'expert', swap(mask))  7.02 us
  transfers between devices with their start and end apart: 6, of which 0 were waited for; matrix products, arithmetic and copies ran while one was open for 0% of the time, Pallas kernels for 34%

profile of v3, /device:TPU:0, one launch (start us, length us, event | category | flops | bytes accessed | tf_op | source)
XLA Modules:
  0.0 102.3 jit_solution(237786473787028770)
XLA Ops:
  0.6 33.9 %layer_two.1 = (bf16[5,192,1536]{2,1,0:T(8,128)(2,1)}, bf16[5,192,1536]{2,1,0:T(8,128)(2,1)}, bf16[5,192,512]{2,1,0:T(8,128)(2,1)}, bf16[5,192,512]{2,1,0:T(8,12...) custom-call(s32[8,64]{1,0:T(8,128)} %bitcast.6, ...), custom_call_target="tpu_custom_call" | custom-call | flops 16000000000 | bytes 37748736 | tf_op jit(solution)/shard_map/layer_two/pallas_call | solution.py:462
  34.5 0.9 collective-permute-start
  35.5 1.0 collective-permute-start.1
  36.4 1.6 %collective-permute-start.2 = (f32[64,1536]{1,0:T(8,128)}, f32[64,1536]{1,0:T(8,128)S(1)}, u32[]{:S(2)}, u32[]{:S(2)}) collective-permute-start(f32[64,1536]{1,0:T(8,128)} %get-tuple-element.37), channel_id=1, source_target_pairs={{0,6},{1,7},{2,4},{3,5},{4,2},{5,3},{6,0},{7,1}} | collective-permute-start | bytes 1179656 | tf_op jit(solution)/shard_map/ppermute | solution.py:544
  38.0 0.0 copy-start
  38.0 0.0 copy-start.1
  38.0 0.0 copy-start.2
  38.0 17.7 %weight_grads.3 = (f32[5,1536,512]{2,1,0:T(8,128)}, f32[5,1536,512]{2,1,0:T(8,128)}, f32[5,512,1536]{2,1,0:T(8,128)}) custom-call(bf16[5,192,1536]{2,1,0:T(8,128)(2,1)} %get-tuple-element.53.u_h, bf16[5,192,1536]{2,1,0:T(8,128)(2,1)} %get-tuple-element.54.z_h, bf16[5,192,512]{2,1,0:T(8,128)(2,1)} %get-tuple-element.55.hid_h, ...), custom_call_target="tpu_custom_call" | custom-call | flops 17999998976 | bytes 58720256 | tf_op jit(solution)/shard_map/weight_grads/pallas_call | solution.py:532
  55.7 0.0 collective-permute-done.r_x
  55.8 0.0 collective-permute-done.1.r_y
  55.8 0.0 collective-permute-done.2.r_d
  55.8 0.0 copy-done
  55.8 0.0 copy-done.1
  55.8 0.0 copy-done.2
  55.8 24.8 %layer_one.1 = (bf16[5,192,1536]{2,1,0:T(8,128)(2,1)}, bf16[5,192,1536]{2,1,0:T(8,128)(2,1)}, bf16[5,192,512]{2,1,0:T(8,128)(2,1)}, bf16[5,192,512]{2,1,0:T(8,12...) custom-call(bf16[64,1536]{1,0:T(8,128)(2,1)S(1)} %copy-done, ...), custom_call_target="tpu_custom_call" | custom-call | flops 16000000000 | bytes 37748736 | tf_op jit(solution)/shard_map/layer_one/pallas_call | solution.py:475
  80.6 0.9 collective-permute-start.3
  81.5 1.0 collective-permute-start.4
  82.5 1.6 %collective-permute-start.5 = (f32[64,1536]{1,0:T(8,128)S(1)}, f32[64,1536]{1,0:T(8,128)S(1)}, u32[]{:S(2)}, u32[]{:S(2)}) collective-permute-start(f32[64,1536]{1,0:T(8,128)S(1)} %get-tuple-element.44), channel_id=1, source_target_pairs={{0,6},{1,7},{2,4},{3,5},{4,2},{5,3},{6,0},{7,1}} | collective-permute-start | bytes 1179656 | tf_op jit(solution)/shard_map/ppermute | solution.py:544
  84.1 17.4 %weight_grads.2 = (f32[5,1536,512]{2,1,0:T(8,128)}, f32[5,1536,512]{2,1,0:T(8,128)}, f32[5,512,1536]{2,1,0:T(8,128)}) custom-call(bf16[5,192,1536]{2,1,0:T(8,128)(2,1)} %get-tuple-element.45.u_h, bf16[5,192,1536]{2,1,0:T(8,128)(2,1)} %get-tuple-element.46.z_h, bf16[5,192,512]{2,1,0:T(8,128)(2,1)} %get-tuple-element.47.hid_h, ...), custom_call_target="tpu_custom_call" | custom-call | flops 17999998976 | bytes 58720256 | tf_op jit(solution)/shard_map/weight_grads/pallas_call | solution.py:532
  101.5 0.0 collective-permute-done.3
  101.5 0.0 collective-permute-done.4
  101.6 0.0 collective-permute-done.5
  101.6 0.8 add_convert_fusion
Async XLA Ops:
  34.5 21.2 %collective-permute-start = (f32[64,1536]{1,0:T(8,128)}, f32[64,1536]{1,0:T(8,128)S(1)}, u32[]{:S(2)}, u32[]{:S(2)}) collective-permute-start(f32[64,1536]{1,0:T(8,128)} %get-tuple-element.35), channel_id=1, source_target_pairs={{0,2},{1,3},{2,0},{3,1},{4,6},{5,7},{6,4},{7,5}} | collective-permute-start | bytes 1179656 | tf_op jit(solution)/shard_map/ppermute | solution.py:544
  35.5 20.3 %collective-permute-start.1 = (f32[64,1536]{1,0:T(8,128)}, f32[64,1536]{1,0:T(8,128)S(1)}, u32[]{:S(2)}, u32[]{:S(2)}) collective-permute-start(f32[64,1536]{1,0:T(8,128)} %get-tuple-element.36), channel_id=1, source_target_pairs={{0,4},{1,5},{2,6},{3,7},{4,0},{5,1},{6,2},{7,3}} | collective-permute-start | bytes 1179656 | tf_op jit(solution)/shard_map/ppermute | solution.py:544
  36.4 19.3 %collective-permute-start.2 = (f32[64,1536]{1,0:T(8,128)}, f32[64,1536]{1,0:T(8,128)S(1)}, u32[]{:S(2)}, u32[]{:S(2)}) collective-permute-start(f32[64,1536]{1,0:T(8,128)} %get-tuple-element.37), channel_id=1, source_target_pairs={{0,6},{1,7},{2,4},{3,5},{4,2},{5,3},{6,0},{7,1}} | collective-permute-start | bytes 1179656 | tf_op jit(solution)/shard_map/ppermute | solution.py:544
  38.0 17.7 %copy-start = (bf16[64,1536]{1,0:T(8,128)(2,1)S(1)}, bf16[64,1536]{1,0:T(8,128)(2,1)}, u32[]{:S(2)}) copy-start(bf16[64,1536]{1,0:T(8,128)(2,1)} %dy_h.1) | copy-start | bytes 589828
  38.0 17.8 %copy-start.1 = (f32[64,1536]{1,0:T(8,128)S(1)}, f32[64,1536]{1,0:T(8,128)}, u32[]{:S(2)}) copy-start(f32[64,1536]{1,0:T(8,128)} %get-tuple-element.34.r_me) | copy-start | bytes 1179652
  38.0 17.8 %copy-start.2 = (f32[32,512]{1,0:T(8,128)S(1)}, f32[32,512]{1,0:T(8,128)}, u32[]{:S(2)}) copy-start(f32[32,512]{1,0:T(8,128)} %get-tuple-element.38.table) | copy-start | bytes 196612
  80.6 21.0 %collective-permute-start.3 = (f32[64,1536]{1,0:T(8,128)S(1)}, f32[64,1536]{1,0:T(8,128)S(1)}, u32[]{:S(2)}, u32[]{:S(2)}) collective-permute-start(f32[64,1536]{1,0:T(8,128)S(1)} %get-tuple-element.42), channel_id=1, source_target_pairs={{0,2},{1,3},{2,0},{3,1},{4,6},{5,7},{6,4},{7,5}} | collective-permute-start | bytes 1179656 | tf_op jit(solution)/shard_map/ppermute | solution.py:544
  81.5 20.0 %collective-permute-start.4 = (f32[64,1536]{1,0:T(8,128)S(1)}, f32[64,1536]{1,0:T(8,128)S(1)}, u32[]{:S(2)}, u32[]{:S(2)}) collective-permute-start(f32[64,1536]{1,0:T(8,128)S(1)} %get-tuple-element.43), channel_id=1, source_target_pairs={{0,4},{1,5},{2,6},{3,7},{4,0},{5,1},{6,2},{7,3}} | collective-permute-start | bytes 1179656 | tf_op jit(solution)/shard_map/ppermute | solution.py:544
  82.5 19.1 %collective-permute-start.5 = (f32[64,1536]{1,0:T(8,128)S(1)}, f32[64,1536]{1,0:T(8,128)S(1)}, u32[]{:S(2)}, u32[]{:S(2)}) collective-permute-start(f32[64,1536]{1,0:T(8,128)S(1)} %get-tuple-element.44), channel_id=1, source_target_pairs={{0,6},{1,7},{2,4},{3,5},{4,2},{5,3},{6,0},{7,1}} | collective-permute-start | bytes 1179656 | tf_op jit(solution)/shard_map/ppermute | solution.py:544

commit v4 on v3

--- a/solution.py
+++ b/solution.py
@@ -192,10 +192,11 @@
 
 
 def row_grads(e, cols, turned, w1, w3, a, b, dxr):
+    dx = jnp.dot(a[e], w1[e, :, cols], preferred_element_type=F32)
     if turned:
-        dx = jnp.dot(a[e], w1[e, :, cols], preferred_element_type=F32) + jnp.dot(b[e], w3[e, :, cols], preferred_element_type=F32)
+        dx = dx + jnp.dot(b[e], w3[e, :, cols], preferred_element_type=F32)
     else:
-        dx = lax.dot_general(a[e], w1[e, cols, :], TRANS_B, preferred_element_type=F32) + lax.dot_general(b[e], w3[e, cols, :], TRANS_B, preferred_element_type=F32)
+        dx = dx + lax.dot_general(b[e], w3[e, cols, :], TRANS_B, preferred_element_type=F32)
     dx = dx.astype(BF16)
     for h in range(2):
         dxr[e * HALF_ROWS : (e + 1) * HALF_ROWS, h * (D // 2) : h * (D // 2) + dx.shape[1]] = dx[h * HALF_ROWS : (h + 1) * HALF_ROWS]
@@ -318,11 +319,11 @@
     gd.start(PARTNER)
     gy.relay_rest(0)
     build_scatter(onehot, scatter)
-    turn(9, 10)
-    gy.relay_rest(1)
     for e in range(LOCAL):
         weights.wait((1,), e)
-    turn(10, 11)
+    turn(9, 12)
+    gy.relay_rest(1)
+    turn(12, 13)
     gy.finish()
     gd.relay_prim(0)
     take_rows(onehot, yall, u)
@@ -337,12 +338,10 @@
     gx.start(PRIM)
     forward(2, 4)
     gx.start(SEC)
+    gd.relay_rest(0)
     forward(4, LOCAL)
-    gd.relay_rest(0)
-    turn(11, 13)
     gd.relay_rest(1)
     turn(13, 3 * LOCAL)
-    gx.relay_prim(0)
     gd.finish()
     gx.start(PARTNER)
     take_rows(onehot, dall, z, gate_col)
@@ -350,9 +349,10 @@
     store_h = pltpu.make_async_copy(hid, hid_o, osem.at[2])
     store_z.start()
     store_h.start()
-    gx.relay_prim(1)
+    gx.relay_prim(0)
     for e in range(LOCAL):
         hidden_grads(e, z, w2t, a, b)
+    gx.relay_prim(1)
     store_a = pltpu.make_async_copy(a, da_o, osem.at[3])
     store_b = pltpu.make_async_copy(b, db_o, osem.at[4])
     store_a.start()
@@ -384,18 +384,20 @@
     load_x = pltpu.make_async_copy(xall_h, xall, lsem.at[0])
     load_x.start()
     weights = Weights((w1_h, w3_h, w2_h), (w1, w3, w2), wsem)
+    weights.start((0, 1), (0,))
     dy1 = (dy_h[...].astype(F32) + ((r_me[...] + r_x[...]) + (r_y[...] + r_d[...]))).astype(BF16)
     dall[pl.ds(pl.multiple_of(ids["me"] * TOK, TOK), TOK), :] = dy1
     dy1_o[...] = dy1
     await_peers()
     gd = Gather(ids, dall, gsend, grecv, 2)
     gd.start(PRIM)
+    build_onehot(table, 16, ids["me"], onehot, gate_col)
     load_x.wait()
-    weights.start((0, 1), (0, 1))
-    build_onehot(table, 16, ids["me"], onehot, gate_col)
+    weights.start((0, 1), (1,))
+    weights.start((2,), (0, 1, 2))
     weights.start((0, 1), (2, 3, 4))
+    weights.start((2,), (3, 4))
     take_rows(onehot, xall, u)
-    weights.start((2,), range(LOCAL))
     gd.start(SEC)
     gd.start(PARTNER)
     build_scatter(onehot, scatter)
@@ -409,16 +411,27 @@
             return carry
         lax.fori_loop(first, last, step, 0)
 
+    def turn(first, last):
+        for i in range(first, last):
+            e = i % LOCAL
+            if i < LOCAL:
+                weights.wait((2,), e)
+                turn_wide(w2, w2t, e)
+            else:
+                turn_tall(w1, w2, e)
+
     forward(0, 1)
     gd.relay_prim(0)
     forward(1, 2)
+    turn(0, 2)
     gd.relay_prim(1)
+    turn(2, 3)
     forward(2, LOCAL)
+    turn(3, 5)
     gd.relay_rest(0)
-    for e in range(LOCAL):
-        weights.wait((2,), e)
-        turn_wide(w2, w2t, e)
+    turn(5, 7)
     gd.relay_rest(1)
+    turn(7, 2 * LOCAL)
     gd.finish()
     take_rows(onehot, dall, z, gate_col)
     store_z = pltpu.make_async_copy(z, z_o, osem.at[1])
@@ -431,7 +444,7 @@
     store_b = pltpu.make_async_copy(b, db_o, osem.at[4])
     store_a.start()
     store_b.start()
-    return_sums(ids, core, x, y, scatter, False, w1, w3, a, b, xall, sums, inbox, xsend, xrecv, ssem, (s_me, s_x, s_y, s_d), lambda n: None)
+    return_sums(ids, core, x, y, scatter, False, w2, w3, a, b, xall, sums, inbox, xsend, xrecv, ssem, (s_me, s_x, s_y, s_d), lambda n: None)
     gd.drain()
     for c in (store_u, store_z, store_h, store_a, store_b):
         c.wait()

time: 102 us -> 99.9 us (0.979)
  Pallas kernels: 93.8 us -> 91.2 us
    pallas_call x1, Pallas kernels: 24.8 us -> 23.1 us  [layer_one(): pl.pallas_call(layer_one_kernel, name='layer_one', out_shape=ROW_OUTS + [...]
  transfers between devices with their start and end apart: 6 -> 6, of which waited for: 0 -> 0; matrix products, arithmetic and copies ran while one was open for 0% -> 0% of each run, Pallas kernels for 34% -> 35%
where the time goes in v4:
time: 99.9 us; the launch traced here: 99.8 us
  Pallas kernels  91.2 us (91%)
  starting transfers between devices  7.02 us (7%)
    pallas_call x2, Pallas kernels, weight_grads(): pl.pallas_call(weight_grad_kernel, name='weight_grads', in_specs=[HBM_SPE...  35.1 us
    pallas_call x1, Pallas kernels, layer_two(): pl.pallas_call(layer_two_kernel, name='layer_two', out_shape=ROW_OUTS + [...  33 us
    pallas_call x1, Pallas kernels, layer_one(): pl.pallas_call(layer_one_kernel, name='layer_one', out_shape=ROW_OUTS + [...  23.1 us
    ppermute x6, starting transfers between devices, exchange_sums(): lax.ppermute(sums[k], 'expert', swap(mask))  7.02 us
  transfers between devices with their start and end apart: 6, of which 0 were waited for; matrix products, arithmetic and copies ran while one was open for 0% of the time, Pallas kernels for 35%

profile of v4, /device:TPU:0, one launch (start us, length us, event | category | flops | bytes accessed | tf_op | source)
XLA Modules:
  0.0 99.8 jit_solution(2698908418213033329)
XLA Ops:
  0.6 33.0 %layer_two.1 = (bf16[5,192,1536]{2,1,0:T(8,128)(2,1)}, bf16[5,192,1536]{2,1,0:T(8,128)(2,1)}, bf16[5,192,512]{2,1,0:T(8,128)(2,1)}, bf16[5,192,512]{2,1,0:T(8,12...) custom-call(s32[8,64]{1,0:T(8,128)} %bitcast.6, ...), custom_call_target="tpu_custom_call" | custom-call | flops 16000000000 | bytes 37748736 | tf_op jit(solution)/shard_map/layer_two/pallas_call | solution.py:475
  33.7 1.1 %collective-permute-start = (f32[64,1536]{1,0:T(8,128)}, f32[64,1536]{1,0:T(8,128)S(1)}, u32[]{:S(2)}, u32[]{:S(2)}) collective-permute-start(f32[64,1536]{1,0:T(8,128)} %get-tuple-element.35), channel_id=1, source_target_pairs={{0,2},{1,3},{2,0},{3,1},{4,6},{5,7},{6,4},{7,5}} | collective-permute-start | bytes 1179656 | tf_op jit(solution)/shard_map/ppermute | solution.py:557
  34.7 0.9 collective-permute-start.1
  35.7 1.5 %collective-permute-start.2 = (f32[64,1536]{1,0:T(8,128)}, f32[64,1536]{1,0:T(8,128)S(1)}, u32[]{:S(2)}, u32[]{:S(2)}) collective-permute-start(f32[64,1536]{1,0:T(8,128)} %get-tuple-element.37), channel_id=1, source_target_pairs={{0,6},{1,7},{2,4},{3,5},{4,2},{5,3},{6,0},{7,1}} | collective-permute-start | bytes 1179656 | tf_op jit(solution)/shard_map/ppermute | solution.py:557
  37.2 0.0 copy-start
  37.2 0.0 copy-start.1
  37.2 0.0 copy-start.2
  37.2 17.7 %weight_grads.3 = (f32[5,1536,512]{2,1,0:T(8,128)}, f32[5,1536,512]{2,1,0:T(8,128)}, f32[5,512,1536]{2,1,0:T(8,128)}) custom-call(bf16[5,192,1536]{2,1,0:T(8,128)(2,1)} %get-tuple-element.53.u_h, bf16[5,192,1536]{2,1,0:T(8,128)(2,1)} %get-tuple-element.54.z_h, bf16[5,192,512]{2,1,0:T(8,128)(2,1)} %get-tuple-element.55.hid_h, ...), custom_call_target="tpu_custom_call" | custom-call | flops 17999998976 | bytes 58720256 | tf_op jit(solution)/shard_map/weight_grads/pallas_call | solution.py:545
  54.9 0.0 collective-permute-done.r_x
  54.9 0.0 collective-permute-done.1.r_y
  54.9 0.0 collective-permute-done.2.r_d
  54.9 0.0 copy-done
  54.9 0.0 copy-done.1
  54.9 0.0 copy-done.2
  55.0 23.1 %layer_one.1 = (bf16[5,192,1536]{2,1,0:T(8,128)(2,1)}, bf16[5,192,1536]{2,1,0:T(8,128)(2,1)}, bf16[5,192,512]{2,1,0:T(8,128)(2,1)}, bf16[5,192,512]{2,1,0:T(8,12...) custom-call(bf16[64,1536]{1,0:T(8,128)(2,1)S(1)} %copy-done, ...), custom_call_target="tpu_custom_call" | custom-call | flops 16000000000 | bytes 37748736 | tf_op jit(solution)/shard_map/layer_one/pallas_call | solution.py:488
  78.0 1.0 %collective-permute-start.3 = (f32[64,1536]{1,0:T(8,128)S(1)}, f32[64,1536]{1,0:T(8,128)S(1)}, u32[]{:S(2)}, u32[]{:S(2)}) collective-permute-start(f32[64,1536]{1,0:T(8,128)S(1)} %get-tuple-element.42), channel_id=1, source_target_pairs={{0,2},{1,3},{2,0},{3,1},{4,6},{5,7},{6,4},{7,5}} | collective-permute-start | bytes 1179656 | tf_op jit(solution)/shard_map/ppermute | solution.py:557
  79.1 1.2 %collective-permute-start.4 = (f32[64,1536]{1,0:T(8,128)S(1)}, f32[64,1536]{1,0:T(8,128)S(1)}, u32[]{:S(2)}, u32[]{:S(2)}) collective-permute-start(f32[64,1536]{1,0:T(8,128)S(1)} %get-tuple-element.43), channel_id=1, source_target_pairs={{0,4},{1,5},{2,6},{3,7},{4,0},{5,1},{6,2},{7,3}} | collective-permute-start | bytes 1179656 | tf_op jit(solution)/shard_map/ppermute | solution.py:557
  80.3 1.3 %collective-permute-start.5 = (f32[64,1536]{1,0:T(8,128)S(1)}, f32[64,1536]{1,0:T(8,128)S(1)}, u32[]{:S(2)}, u32[]{:S(2)}) collective-permute-start(f32[64,1536]{1,0:T(8,128)S(1)} %get-tuple-element.44), channel_id=1, source_target_pairs={{0,6},{1,7},{2,4},{3,5},{4,2},{5,3},{6,0},{7,1}} | collective-permute-start | bytes 1179656 | tf_op jit(solution)/shard_map/ppermute | solution.py:557
  81.6 17.4 %weight_grads.2 = (f32[5,1536,512]{2,1,0:T(8,128)}, f32[5,1536,512]{2,1,0:T(8,128)}, f32[5,512,1536]{2,1,0:T(8,128)}) custom-call(bf16[5,192,1536]{2,1,0:T(8,128)(2,1)} %get-tuple-element.45.u_h, bf16[5,192,1536]{2,1,0:T(8,128)(2,1)} %get-tuple-element.46.z_h, bf16[5,192,512]{2,1,0:T(8,128)(2,1)} %get-tuple-element.47.hid_h, ...), custom_call_target="tpu_custom_call" | custom-call | flops 17999998976 | bytes 58720256 | tf_op jit(solution)/shard_map/weight_grads/pallas_call | solution.py:545
  99.0 0.0 collective-permute-done.3
  99.0 0.0 collective-permute-done.4
  99.0 0.0 collective-permute-done.5
  99.0 0.8 add_convert_fusion
Async XLA Ops:
  33.7 21.2 %collective-permute-start = (f32[64,1536]{1,0:T(8,128)}, f32[64,1536]{1,0:T(8,128)S(1)}, u32[]{:S(2)}, u32[]{:S(2)}) collective-permute-start(f32[64,1536]{1,0:T(8,128)} %get-tuple-element.35), channel_id=1, source_target_pairs={{0,2},{1,3},{2,0},{3,1},{4,6},{5,7},{6,4},{7,5}} | collective-permute-start | bytes 1179656 | tf_op jit(solution)/shard_map/ppermute | solution.py:557
  34.7 20.2 %collective-permute-start.1 = (f32[64,1536]{1,0:T(8,128)}, f32[64,1536]{1,0:T(8,128)S(1)}, u32[]{:S(2)}, u32[]{:S(2)}) collective-permute-start(f32[64,1536]{1,0:T(8,128)} %get-tuple-element.36), channel_id=1, source_target_pairs={{0,4},{1,5},{2,6},{3,7},{4,0},{5,1},{6,2},{7,3}} | collective-permute-start | bytes 1179656 | tf_op jit(solution)/shard_map/ppermute | solution.py:557
  35.7 19.2 %collective-permute-start.2 = (f32[64,1536]{1,0:T(8,128)}, f32[64,1536]{1,0:T(8,128)S(1)}, u32[]{:S(2)}, u32[]{:S(2)}) collective-permute-start(f32[64,1536]{1,0:T(8,128)} %get-tuple-element.37), channel_id=1, source_target_pairs={{0,6},{1,7},{2,4},{3,5},{4,2},{5,3},{6,0},{7,1}} | collective-permute-start | bytes 1179656 | tf_op jit(solution)/shard_map/ppermute | solution.py:557
  37.2 17.7 %copy-start = (bf16[64,1536]{1,0:T(8,128)(2,1)S(1)}, bf16[64,1536]{1,0:T(8,128)(2,1)}, u32[]{:S(2)}) copy-start(bf16[64,1536]{1,0:T(8,128)(2,1)} %dy_h.1) | copy-start | bytes 589828
  37.2 17.8 %copy-start.1 = (f32[64,1536]{1,0:T(8,128)S(1)}, f32[64,1536]{1,0:T(8,128)}, u32[]{:S(2)}) copy-start(f32[64,1536]{1,0:T(8,128)} %get-tuple-element.34.r_me) | copy-start | bytes 1179652
  37.2 17.8 %copy-start.2 = (f32[32,512]{1,0:T(8,128)S(1)}, f32[32,512]{1,0:T(8,128)}, u32[]{:S(2)}) copy-start(f32[32,512]{1,0:T(8,128)} %get-tuple-element.38.table) | copy-start | bytes 196612
  78.0 21.0 %collective-permute-start.3 = (f32[64,1536]{1,0:T(8,128)S(1)}, f32[64,1536]{1,0:T(8,128)S(1)}, u32[]{:S(2)}, u32[]{:S(2)}) collective-permute-start(f32[64,1536]{1,0:T(8,128)S(1)} %get-tuple-element.42), channel_id=1, source_target_pairs={{0,2},{1,3},{2,0},{3,1},{4,6},{5,7},{6,4},{7,5}} | collective-permute-start | bytes 1179656 | tf_op jit(solution)/shard_map/ppermute | solution.py:557
  79.1 19.9 %collective-permute-start.4 = (f32[64,1536]{1,0:T(8,128)S(1)}, f32[64,1536]{1,0:T(8,128)S(1)}, u32[]{:S(2)}, u32[]{:S(2)}) collective-permute-start(f32[64,1536]{1,0:T(8,128)S(1)} %get-tuple-element.43), channel_id=1, source_target_pairs={{0,4},{1,5},{2,6},{3,7},{4,0},{5,1},{6,2},{7,3}} | collective-permute-start | bytes 1179656 | tf_op jit(solution)/shard_map/ppermute | solution.py:557
  80.3 18.8 %collective-permute-start.5 = (f32[64,1536]{1,0:T(8,128)S(1)}, f32[64,1536]{1,0:T(8,128)S(1)}, u32[]{:S(2)}, u32[]{:S(2)}) collective-permute-start(f32[64,1536]{1,0:T(8,128)S(1)} %get-tuple-element.44), channel_id=1, source_target_pairs={{0,6},{1,7},{2,4},{3,5},{4,2},{5,3},{6,0},{7,1}} | collective-permute-start | bytes 1179656 | tf_op jit(solution)/shard_map/ppermute | solution.py:557

commit v5 on v4

--- a/solution.py
+++ b/solution.py
@@ -18,6 +18,7 @@
 ROWS = 8 * CAP
 STEP = 512
 SLOTS = 512
+TURNED = 5
 CHUNKS = ((0, 768), (768, 512), (1280, 256))
 
 
@@ -191,9 +192,12 @@
     b[e] = (dh * (act * sig)).astype(BF16)
 
 
-def row_grads(e, cols, turned, w1, w3, a, b, dxr):
-    dx = jnp.dot(a[e], w1[e, :, cols], preferred_element_type=F32)
-    if turned:
+def row_grads(e, cols, turned, w1t, w1, w3, a, b, dxr):
+    if turned is None or e < turned:
+        dx = jnp.dot(a[e], w1t[e, :, cols], preferred_element_type=F32)
+    else:
+        dx = lax.dot_general(a[e], w1[e, cols, :], TRANS_B, preferred_element_type=F32)
+    if turned is None:
         dx = dx + jnp.dot(b[e], w3[e, :, cols], preferred_element_type=F32)
     else:
         dx = dx + lax.dot_general(b[e], w3[e, cols, :], TRANS_B, preferred_element_type=F32)
@@ -202,7 +206,7 @@
         dxr[e * HALF_ROWS : (e + 1) * HALF_ROWS, h * (D // 2) : h * (D // 2) + dx.shape[1]] = dx[h * HALF_ROWS : (h + 1) * HALF_ROWS]
 
 
-def return_sums(ids, core, x, y, scatter, turned, w1, w3, a, b, dxr, sums, inbox, send, recv, ssem, outs, between):
+def return_sums(ids, core, x, y, scatter, turned, w1t, w1, w3, a, b, dxr, sums, inbox, send, recv, ssem, outs, between):
     def exchange(n, yy, xx):
         theirs = 4 * yy + 2 * xx + (1 - core)
         cols = pl.ds(*CHUNKS[n])
@@ -228,7 +232,7 @@
     for n in range(len(CHUNKS)):
         cols = slice(CHUNKS[n][0], sum(CHUNKS[n]))
         for e in range(LOCAL):
-            row_grads(e, cols, turned, w1, w3, a, b, dxr)
+            row_grads(e, cols, turned, w1t, w1, w3, a, b, dxr)
         for h in range(2):
             sums[h * 256 : (h + 1) * 256, cols] = jnp.dot(scatter[h, :, 0 : LOCAL * HALF_ROWS], dxr[0 : LOCAL * HALF_ROWS, h * (D // 2) : h * (D // 2) + CHUNKS[n][1]], preferred_element_type=F32)
         for k in range(4):
@@ -285,9 +289,9 @@
     gt.start(SEC)
     gy.start(PRIM)
     gt.start(PARTNER)
+    weights.start((2,), range(LOCAL))
     for c in local[1:]:
         c.wait()
-    weights.start((2,), range(LOCAL))
     weights.start((0, 1), range(LOCAL))
 
     def turn(first, last):
@@ -368,7 +372,7 @@
             store_x.start()
 
     gy.drain()
-    return_sums(ids, core, x, y, scatter, True, w2, w3t, a, b, yall, sums, inbox, xsend, xrecv, ssem, (s_me, s_x, s_y, s_d), between)
+    return_sums(ids, core, x, y, scatter, None, w2, None, w3t, a, b, yall, sums, inbox, xsend, xrecv, ssem, (s_me, s_x, s_y, s_d), between)
     for g in (gt, gd, gx):
         g.drain()
     for c in (store_u, store_z, store_h, store_a, store_b, store_x, save_table):
@@ -391,12 +395,13 @@
     await_peers()
     gd = Gather(ids, dall, gsend, grecv, 2)
     gd.start(PRIM)
+    weights.start((2,), (0, 1))
     build_onehot(table, 16, ids["me"], onehot, gate_col)
     load_x.wait()
     weights.start((0, 1), (1,))
-    weights.start((2,), (0, 1, 2))
+    weights.start((2,), (2, 3))
     weights.start((0, 1), (2, 3, 4))
-    weights.start((2,), (3, 4))
+    weights.start((2,), (4,))
     take_rows(onehot, xall, u)
     gd.start(SEC)
     gd.start(PARTNER)
@@ -421,17 +426,17 @@
                 turn_tall(w1, w2, e)
 
     forward(0, 1)
+    turn(0, 2)
     gd.relay_prim(0)
     forward(1, 2)
-    turn(0, 2)
+    turn(2, 4)
     gd.relay_prim(1)
-    turn(2, 3)
     forward(2, LOCAL)
-    turn(3, 5)
+    turn(4, 5)
     gd.relay_rest(0)
     turn(5, 7)
     gd.relay_rest(1)
-    turn(7, 2 * LOCAL)
+    turn(7, LOCAL + TURNED)
     gd.finish()
     take_rows(onehot, dall, z, gate_col)
     store_z = pltpu.make_async_copy(z, z_o, osem.at[1])
@@ -444,7 +449,7 @@
     store_b = pltpu.make_async_copy(b, db_o, osem.at[4])
     store_a.start()
     store_b.start()
-    return_sums(ids, core, x, y, scatter, False, w2, w3, a, b, xall, sums, inbox, xsend, xrecv, ssem, (s_me, s_x, s_y, s_d), lambda n: None)
+    return_sums(ids, core, x, y, scatter, TURNED, w2, w1, w3, a, b, xall, sums, inbox, xsend, xrecv, ssem, (s_me, s_x, s_y, s_d), lambda n: None)
     gd.drain()
     for c in (store_u, store_z, store_h, store_a, store_b):
         c.wait()

time: 99.9 us -> 99.5 us (level)
  no operation moved by 1% of the time
where the time goes in v5:
time: 99.5 us; the launch traced here: 99.3 us
  Pallas kernels  90.8 us (91%)
  starting transfers between devices  7.02 us (7%)
    pallas_call x2, Pallas kernels, weight_grads(): pl.pallas_call(weight_grad_kernel, name='weight_grads', in_specs=[HBM_SPE...  35.1 us
    pallas_call x1, Pallas kernels, layer_two(): pl.pallas_call(layer_two_kernel, name='layer_two', out_shape=ROW_OUTS + [...  33 us
    pallas_call x1, Pallas kernels, layer_one(): pl.pallas_call(layer_one_kernel, name='layer_one', out_shape=ROW_OUTS + [...  22.6 us
    ppermute x6, starting transfers between devices, exchange_sums(): lax.ppermute(sums[k], 'expert', swap(mask))  7.02 us
  transfers between devices with their start and end apart: 6, of which 0 were waited for; matrix products, arithmetic and copies ran while one was open for 0% of the time, Pallas kernels for 35%

profile of v5, /device:TPU:0, one launch (start us, length us, event | category | flops | bytes accessed | tf_op | source)
XLA Modules:
  0.0 99.3 jit_solution(14838671026157691993)
XLA Ops:
  0.6 33.0 %layer_two.1 = (bf16[5,192,1536]{2,1,0:T(8,128)(2,1)}, bf16[5,192,1536]{2,1,0:T(8,128)(2,1)}, bf16[5,192,512]{2,1,0:T(8,128)(2,1)}, bf16[5,192,512]{2,1,0:T(8,12...) custom-call(s32[8,64]{1,0:T(8,128)} %bitcast.6, ...), custom_call_target="tpu_custom_call" | custom-call | flops 16000000000 | bytes 37748736 | tf_op jit(solution)/shard_map/layer_two/pallas_call | solution.py:480
  33.7 0.9 collective-permute-start
  34.6 1.1 %collective-permute-start.1 = (f32[64,1536]{1,0:T(8,128)}, f32[64,1536]{1,0:T(8,128)S(1)}, u32[]{:S(2)}, u32[]{:S(2)}) collective-permute-start(f32[64,1536]{1,0:T(8,128)} %get-tuple-element.36), channel_id=1, source_target_pairs={{0,4},{1,5},{2,6},{3,7},{4,0},{5,1},{6,2},{7,3}} | collective-permute-start | bytes 1179656 | tf_op jit(solution)/shard_map/ppermute | solution.py:562
  35.7 1.5 %collective-permute-start.2 = (f32[64,1536]{1,0:T(8,128)}, f32[64,1536]{1,0:T(8,128)S(1)}, u32[]{:S(2)}, u32[]{:S(2)}) collective-permute-start(f32[64,1536]{1,0:T(8,128)} %get-tuple-element.37), channel_id=1, source_target_pairs={{0,6},{1,7},{2,4},{3,5},{4,2},{5,3},{6,0},{7,1}} | collective-permute-start | bytes 1179656 | tf_op jit(solution)/shard_map/ppermute | solution.py:562
  37.2 0.0 copy-start
  37.2 0.0 copy-start.1
  37.2 0.0 copy-start.2
  37.2 17.7 %weight_grads.3 = (f32[5,1536,512]{2,1,0:T(8,128)}, f32[5,1536,512]{2,1,0:T(8,128)}, f32[5,512,1536]{2,1,0:T(8,128)}) custom-call(bf16[5,192,1536]{2,1,0:T(8,128)(2,1)} %get-tuple-element.53.u_h, bf16[5,192,1536]{2,1,0:T(8,128)(2,1)} %get-tuple-element.54.z_h, bf16[5,192,512]{2,1,0:T(8,128)(2,1)} %get-tuple-element.55.hid_h, ...), custom_call_target="tpu_custom_call" | custom-call | flops 17999998976 | bytes 58720256 | tf_op jit(solution)/shard_map/weight_grads/pallas_call | solution.py:550
  54.9 0.0 collective-permute-done.r_x
  54.9 0.0 collective-permute-done.1.r_y
  54.9 0.0 collective-permute-done.2.r_d
  54.9 0.0 copy-done
  54.9 0.0 copy-done.1
  54.9 0.0 copy-done.2
  54.9 22.6 %layer_one.1 = (bf16[5,192,1536]{2,1,0:T(8,128)(2,1)}, bf16[5,192,1536]{2,1,0:T(8,128)(2,1)}, bf16[5,192,512]{2,1,0:T(8,128)(2,1)}, bf16[5,192,512]{2,1,0:T(8,12...) custom-call(bf16[64,1536]{1,0:T(8,128)(2,1)S(1)} %copy-done, ...), custom_call_target="tpu_custom_call" | custom-call | flops 16000000000 | bytes 37748736 | tf_op jit(solution)/shard_map/layer_one/pallas_call | solution.py:493
  77.6 1.1 %collective-permute-start.3 = (f32[64,1536]{1,0:T(8,128)S(1)}, f32[64,1536]{1,0:T(8,128)S(1)}, u32[]{:S(2)}, u32[]{:S(2)}) collective-permute-start(f32[64,1536]{1,0:T(8,128)S(1)} %get-tuple-element.42), channel_id=1, source_target_pairs={{0,2},{1,3},{2,0},{3,1},{4,6},{5,7},{6,4},{7,5}} | collective-permute-start | bytes 1179656 | tf_op jit(solution)/shard_map/ppermute | solution.py:562
  78.7 0.9 collective-permute-start.4
  79.6 1.5 %collective-permute-start.5 = (f32[64,1536]{1,0:T(8,128)S(1)}, f32[64,1536]{1,0:T(8,128)S(1)}, u32[]{:S(2)}, u32[]{:S(2)}) collective-permute-start(f32[64,1536]{1,0:T(8,128)S(1)} %get-tuple-element.44), channel_id=1, source_target_pairs={{0,6},{1,7},{2,4},{3,5},{4,2},{5,3},{6,0},{7,1}} | collective-permute-start | bytes 1179656 | tf_op jit(solution)/shard_map/ppermute | solution.py:562
  81.1 17.4 %weight_grads.2 = (f32[5,1536,512]{2,1,0:T(8,128)}, f32[5,1536,512]{2,1,0:T(8,128)}, f32[5,512,1536]{2,1,0:T(8,128)}) custom-call(bf16[5,192,1536]{2,1,0:T(8,128)(2,1)} %get-tuple-element.45.u_h, bf16[5,192,1536]{2,1,0:T(8,128)(2,1)} %get-tuple-element.46.z_h, bf16[5,192,512]{2,1,0:T(8,128)(2,1)} %get-tuple-element.47.hid_h, ...), custom_call_target="tpu_custom_call" | custom-call | flops 17999998976 | bytes 58720256 | tf_op jit(solution)/shard_map/weight_grads/pallas_call | solution.py:550
  98.5 0.0 collective-permute-done.3
  98.5 0.0 collective-permute-done.4
  98.6 0.0 collective-permute-done.5
  98.6 0.8 add_convert_fusion
Async XLA Ops:
  33.7 21.2 %collective-permute-start = (f32[64,1536]{1,0:T(8,128)}, f32[64,1536]{1,0:T(8,128)S(1)}, u32[]{:S(2)}, u32[]{:S(2)}) collective-permute-start(f32[64,1536]{1,0:T(8,128)} %get-tuple-element.35), channel_id=1, source_target_pairs={{0,2},{1,3},{2,0},{3,1},{4,6},{5,7},{6,4},{7,5}} | collective-permute-start | bytes 1179656 | tf_op jit(solution)/shard_map/ppermute | solution.py:562
  34.6 20.3 %collective-permute-start.1 = (f32[64,1536]{1,0:T(8,128)}, f32[64,1536]{1,0:T(8,128)S(1)}, u32[]{:S(2)}, u32[]{:S(2)}) collective-permute-start(f32[64,1536]{1,0:T(8,128)} %get-tuple-element.36), channel_id=1, source_target_pairs={{0,4},{1,5},{2,6},{3,7},{4,0},{5,1},{6,2},{7,3}} | collective-permute-start | bytes 1179656 | tf_op jit(solution)/shard_map/ppermute | solution.py:562
  35.7 19.2 %collective-permute-start.2 = (f32[64,1536]{1,0:T(8,128)}, f32[64,1536]{1,0:T(8,128)S(1)}, u32[]{:S(2)}, u32[]{:S(2)}) collective-permute-start(f32[64,1536]{1,0:T(8,128)} %get-tuple-element.37), channel_id=1, source_target_pairs={{0,6},{1,7},{2,4},{3,5},{4,2},{5,3},{6,0},{7,1}} | collective-permute-start | bytes 1179656 | tf_op jit(solution)/shard_map/ppermute | solution.py:562
  37.2 17.7 %copy-start = (bf16[64,1536]{1,0:T(8,128)(2,1)S(1)}, bf16[64,1536]{1,0:T(8,128)(2,1)}, u32[]{:S(2)}) copy-start(bf16[64,1536]{1,0:T(8,128)(2,1)} %dy_h.1) | copy-start | bytes 589828
  37.2 17.8 %copy-start.1 = (f32[64,1536]{1,0:T(8,128)S(1)}, f32[64,1536]{1,0:T(8,128)}, u32[]{:S(2)}) copy-start(f32[64,1536]{1,0:T(8,128)} %get-tuple-element.34.r_me) | copy-start | bytes 1179652
  37.2 17.8 %copy-start.2 = (f32[32,512]{1,0:T(8,128)S(1)}, f32[32,512]{1,0:T(8,128)}, u32[]{:S(2)}) copy-start(f32[32,512]{1,0:T(8,128)} %get-tuple-element.38.table) | copy-start | bytes 196612
  77.6 21.0 %collective-permute-start.3 = (f32[64,1536]{1,0:T(8,128)S(1)}, f32[64,1536]{1,0:T(8,128)S(1)}, u32[]{:S(2)}, u32[]{:S(2)}) collective-permute-start(f32[64,1536]{1,0:T(8,128)S(1)} %get-tuple-element.42), channel_id=1, source_target_pairs={{0,2},{1,3},{2,0},{3,1},{4,6},{5,7},{6,4},{7,5}} | collective-permute-start | bytes 1179656 | tf_op jit(solution)/shard_map/ppermute | solution.py:562
  78.7 19.9 %collective-permute-start.4 = (f32[64,1536]{1,0:T(8,128)S(1)}, f32[64,1536]{1,0:T(8,128)S(1)}, u32[]{:S(2)}, u32[]{:S(2)}) collective-permute-start(f32[64,1536]{1,0:T(8,128)S(1)} %get-tuple-element.43), channel_id=1, source_target_pairs={{0,4},{1,5},{2,6},{3,7},{4,0},{5,1},{6,2},{7,3}} | collective-permute-start | bytes 1179656 | tf_op jit(solution)/shard_map/ppermute | solution.py:562
  79.6 18.9 %collective-permute-start.5 = (f32[64,1536]{1,0:T(8,128)S(1)}, f32[64,1536]{1,0:T(8,128)S(1)}, u32[]{:S(2)}, u32[]{:S(2)}) collective-permute-start(f32[64,1536]{1,0:T(8,128)S(1)} %get-tuple-element.44), channel_id=1, source_target_pairs={{0,6},{1,7},{2,4},{3,5},{4,2},{5,3},{6,0},{7,1}} | collective-permute-start | bytes 1179656 | tf_op jit(solution)/shard_map/ppermute | solution.py:562

commit v6 on v5

--- a/solution.py
+++ b/solution.py
@@ -559,7 +559,7 @@
 
 def exchange_sums(sums):
     swap = lambda mask: [(i, i ^ mask) for i in range(8)]
-    return (sums[0],) + tuple(lax.ppermute(sums[k], "expert", swap(mask)) for k, mask in ((1, 2), (2, 4), (3, 6)))
+    return (sums[0],) + tuple(lax.ppermute(sums[k], "expert", swap(mask)) for k, mask in ((3, 6), (1, 2), (2, 4)))
 
 
 def solution(mesh):

time: 99.5 us -> 99.5 us (level)
  no operation moved by 1% of the time
where the time goes in v6:
time: 99.5 us; the launch traced here: 99.3 us
  Pallas kernels  90.8 us (91%)
  starting transfers between devices  7.02 us (7%)
    pallas_call x2, Pallas kernels, weight_grads(): pl.pallas_call(weight_grad_kernel, name='weight_grads', in_specs=[HBM_SPE...  35.1 us
    pallas_call x1, Pallas kernels, layer_two(): pl.pallas_call(layer_two_kernel, name='layer_two', out_shape=ROW_OUTS + [...  33 us
    pallas_call x1, Pallas kernels, layer_one(): pl.pallas_call(layer_one_kernel, name='layer_one', out_shape=ROW_OUTS + [...  22.6 us
    ppermute x6, starting transfers between devices, exchange_sums(): lax.ppermute(sums[k], 'expert', swap(mask))  7.02 us
  transfers between devices with their start and end apart: 6, of which 0 were waited for; matrix products, arithmetic and copies ran while one was open for 0% of the time, Pallas kernels for 35%

profile of v6, /device:TPU:0, one launch (start us, length us, event | category | flops | bytes accessed | tf_op | source)
XLA Modules:
  0.0 99.3 jit_solution(885881414560420773)
XLA Ops:
  0.6 33.0 %layer_two.1 = (bf16[5,192,1536]{2,1,0:T(8,128)(2,1)}, bf16[5,192,1536]{2,1,0:T(8,128)(2,1)}, bf16[5,192,512]{2,1,0:T(8,128)(2,1)}, bf16[5,192,512]{2,1,0:T(8,12...) custom-call(s32[8,64]{1,0:T(8,128)} %bitcast.6, ...), custom_call_target="tpu_custom_call" | custom-call | flops 16000000000 | bytes 37748736 | tf_op jit(solution)/shard_map/layer_two/pallas_call | solution.py:480
  33.7 1.5 %collective-permute-start = (f32[64,1536]{1,0:T(8,128)}, f32[64,1536]{1,0:T(8,128)S(1)}, u32[]{:S(2)}, u32[]{:S(2)}) collective-permute-start(f32[64,1536]{1,0:T(8,128)} %get-tuple-element.35), channel_id=1, source_target_pairs={{0,6},{1,7},{2,4},{3,5},{4,2},{5,3},{6,0},{7,1}} | collective-permute-start | bytes 1179656 | tf_op jit(solution)/shard_map/ppermute | solution.py:562
  35.1 0.7 collective-permute-start.1
  35.8 1.3 %collective-permute-start.2 = (f32[64,1536]{1,0:T(8,128)}, f32[64,1536]{1,0:T(8,128)S(1)}, u32[]{:S(2)}, u32[]{:S(2)}) collective-permute-start(f32[64,1536]{1,0:T(8,128)} %get-tuple-element.37), channel_id=1, source_target_pairs={{0,4},{1,5},{2,6},{3,7},{4,0},{5,1},{6,2},{7,3}} | collective-permute-start | bytes 1179656 | tf_op jit(solution)/shard_map/ppermute | solution.py:562
  37.2 0.0 copy-start
  37.2 0.0 copy-start.1
  37.2 0.0 copy-start.2
  37.2 17.7 %weight_grads.3 = (f32[5,1536,512]{2,1,0:T(8,128)}, f32[5,1536,512]{2,1,0:T(8,128)}, f32[5,512,1536]{2,1,0:T(8,128)}) custom-call(bf16[5,192,1536]{2,1,0:T(8,128)(2,1)} %get-tuple-element.53.u_h, bf16[5,192,1536]{2,1,0:T(8,128)(2,1)} %get-tuple-element.54.z_h, bf16[5,192,512]{2,1,0:T(8,128)(2,1)} %get-tuple-element.55.hid_h, ...), custom_call_target="tpu_custom_call" | custom-call | flops 17999998976 | bytes 58720256 | tf_op jit(solution)/shard_map/weight_grads/pallas_call | solution.py:550
  54.9 0.0 collective-permute-done.r_x
  54.9 0.0 collective-permute-done.1.r_y
  54.9 0.0 collective-permute-done.2.r_d
  54.9 0.0 copy-done
  54.9 0.0 copy-done.1
  54.9 0.0 copy-done.2
  54.9 22.6 %layer_one.1 = (bf16[5,192,1536]{2,1,0:T(8,128)(2,1)}, bf16[5,192,1536]{2,1,0:T(8,128)(2,1)}, bf16[5,192,512]{2,1,0:T(8,128)(2,1)}, bf16[5,192,512]{2,1,0:T(8,12...) custom-call(bf16[64,1536]{1,0:T(8,128)(2,1)S(1)} %copy-done, ...), custom_call_target="tpu_custom_call" | custom-call | flops 16000000000 | bytes 37748736 | tf_op jit(solution)/shard_map/layer_one/pallas_call | solution.py:493
  77.6 1.5 %collective-permute-start.3 = (f32[64,1536]{1,0:T(8,128)S(1)}, f32[64,1536]{1,0:T(8,128)S(1)}, u32[]{:S(2)}, u32[]{:S(2)}) collective-permute-start(f32[64,1536]{1,0:T(8,128)S(1)} %get-tuple-element.42), channel_id=1, source_target_pairs={{0,6},{1,7},{2,4},{3,5},{4,2},{5,3},{6,0},{7,1}} | collective-permute-start | bytes 1179656 | tf_op jit(solution)/shard_map/ppermute | solution.py:562
  79.1 1.1 %collective-permute-start.4 = (f32[64,1536]{1,0:T(8,128)S(1)}, f32[64,1536]{1,0:T(8,128)S(1)}, u32[]{:S(2)}, u32[]{:S(2)}) collective-permute-start(f32[64,1536]{1,0:T(8,128)S(1)} %get-tuple-element.43), channel_id=1, source_target_pairs={{0,2},{1,3},{2,0},{3,1},{4,6},{5,7},{6,4},{7,5}} | collective-permute-start | bytes 1179656 | tf_op jit(solution)/shard_map/ppermute | solution.py:562
  80.1 1.0 collective-permute-start.5
  81.1 17.4 %weight_grads.2 = (f32[5,1536,512]{2,1,0:T(8,128)}, f32[5,1536,512]{2,1,0:T(8,128)}, f32[5,512,1536]{2,1,0:T(8,128)}) custom-call(bf16[5,192,1536]{2,1,0:T(8,128)(2,1)} %get-tuple-element.45.u_h, bf16[5,192,1536]{2,1,0:T(8,128)(2,1)} %get-tuple-element.46.z_h, bf16[5,192,512]{2,1,0:T(8,128)(2,1)} %get-tuple-element.47.hid_h, ...), custom_call_target="tpu_custom_call" | custom-call | flops 17999998976 | bytes 58720256 | tf_op jit(solution)/shard_map/weight_grads/pallas_call | solution.py:550
  98.5 0.0 collective-permute-done.3
  98.5 0.0 collective-permute-done.4
  98.5 0.0 collective-permute-done.5
  98.6 0.8 add_convert_fusion
Async XLA Ops:
  33.7 21.2 %collective-permute-start = (f32[64,1536]{1,0:T(8,128)}, f32[64,1536]{1,0:T(8,128)S(1)}, u32[]{:S(2)}, u32[]{:S(2)}) collective-permute-start(f32[64,1536]{1,0:T(8,128)} %get-tuple-element.35), channel_id=1, source_target_pairs={{0,6},{1,7},{2,4},{3,5},{4,2},{5,3},{6,0},{7,1}} | collective-permute-start | bytes 1179656 | tf_op jit(solution)/shard_map/ppermute | solution.py:562
  35.1 19.8 %collective-permute-start.1 = (f32[64,1536]{1,0:T(8,128)}, f32[64,1536]{1,0:T(8,128)S(1)}, u32[]{:S(2)}, u32[]{:S(2)}) collective-permute-start(f32[64,1536]{1,0:T(8,128)} %get-tuple-element.36), channel_id=1, source_target_pairs={{0,2},{1,3},{2,0},{3,1},{4,6},{5,7},{6,4},{7,5}} | collective-permute-start | bytes 1179656 | tf_op jit(solution)/shard_map/ppermute | solution.py:562
  35.8 19.1 %collective-permute-start.2 = (f32[64,1536]{1,0:T(8,128)}, f32[64,1536]{1,0:T(8,128)S(1)}, u32[]{:S(2)}, u32[]{:S(2)}) collective-permute-start(f32[64,1536]{1,0:T(8,128)} %get-tuple-element.37), channel_id=1, source_target_pairs={{0,4},{1,5},{2,6},{3,7},{4,0},{5,1},{6,2},{7,3}} | collective-permute-start | bytes 1179656 | tf_op jit(solution)/shard_map/ppermute | solution.py:562
  37.2 17.7 %copy-start = (bf16[64,1536]{1,0:T(8,128)(2,1)S(1)}, bf16[64,1536]{1,0:T(8,128)(2,1)}, u32[]{:S(2)}) copy-start(bf16[64,1536]{1,0:T(8,128)(2,1)} %dy_h.1) | copy-start | bytes 589828
  37.2 17.8 %copy-start.1 = (f32[64,1536]{1,0:T(8,128)S(1)}, f32[64,1536]{1,0:T(8,128)}, u32[]{:S(2)}) copy-start(f32[64,1536]{1,0:T(8,128)} %get-tuple-element.34.r_me) | copy-start | bytes 1179652
  37.2 17.8 %copy-start.2 = (f32[32,512]{1,0:T(8,128)S(1)}, f32[32,512]{1,0:T(8,128)}, u32[]{:S(2)}) copy-start(f32[32,512]{1,0:T(8,128)} %get-tuple-element.38.table) | copy-start | bytes 196612
  77.6 21.0 %collective-permute-start.3 = (f32[64,1536]{1,0:T(8,128)S(1)}, f32[64,1536]{1,0:T(8,128)S(1)}, u32[]{:S(2)}, u32[]{:S(2)}) collective-permute-start(f32[64,1536]{1,0:T(8,128)S(1)} %get-tuple-element.42), channel_id=1, source_target_pairs={{0,6},{1,7},{2,4},{3,5},{4,2},{5,3},{6,0},{7,1}} | collective-permute-start | bytes 1179656 | tf_op jit(solution)/shard_map/ppermute | solution.py:562
  79.1 19.5 %collective-permute-start.4 = (f32[64,1536]{1,0:T(8,128)S(1)}, f32[64,1536]{1,0:T(8,128)S(1)}, u32[]{:S(2)}, u32[]{:S(2)}) collective-permute-start(f32[64,1536]{1,0:T(8,128)S(1)} %get-tuple-element.43), channel_id=1, source_target_pairs={{0,2},{1,3},{2,0},{3,1},{4,6},{5,7},{6,4},{7,5}} | collective-permute-start | bytes 1179656 | tf_op jit(solution)/shard_map/ppermute | solution.py:562
  80.1 18.4 %collective-permute-start.5 = (f32[64,1536]{1,0:T(8,128)S(1)}, f32[64,1536]{1,0:T(8,128)S(1)}, u32[]{:S(2)}, u32[]{:S(2)}) collective-permute-start(f32[64,1536]{1,0:T(8,128)S(1)} %get-tuple-element.44), channel_id=1, source_target_pairs={{0,4},{1,5},{2,6},{3,7},{4,0},{5,1},{6,2},{7,3}} | collective-permute-start | bytes 1179656 | tf_op jit(solution)/shard_map/ppermute | solution.py:562
